TPU v7x, 8 devices: a whole 2x2x1 slice. The times are simulated.
8 devices in a mesh: dp: 1 (over z), sp: 8 (over y, x, core).
Axes of the slice: x: 2, y: 2, z: 1, core: 2. Of those that a mesh axis runs over, the one named last changes fastest.
Arguments:
- hidden: bfloat16 [8, 1024, 2048], P('dp', 'sp')
- norm_w: bfloat16 [2048], replicated
- w_qkv: bfloat16 [2048, 3072], replicated
- w_out: bfloat16 [32, 64, 2048], replicated
- long_factor: float32 [32], replicated
- grad_out: bfloat16 [8, 1024, 2048], P('dp', 'sp')
Outputs:
- output 1: bfloat16 [8, 1024, 2048], P('dp', 'sp')
- output 2: bfloat16 [8, 1024, 2048], P('dp', 'sp')
- output 3: float32 [2048, 3072], P('dp')
- output 4: float32 [32, 64, 2048], P('dp')
- output 5: float32 [2048], P('dp')
All inputs are finite; a program needn't handle non-finite values.
Results may differ from a plain program's by a relative error of at most 0.0104923.
Values are sent between devices in bfloat16 or wider.
A program may use at most 1 GiB of HBM per device.

v0:
```python
import math
import functools
import jax
import jax.numpy as jnp
from jax import lax
from jax.sharding import PartitionSpec as P, NamedSharding

NORM_EPS = 1e-5
ROPE_BASE = 10000.0
ROPE_GAIN = math.sqrt(1.0 + math.log(32.0) / math.log(4096.0))
MASK_VALUE = -1e30


def rope_tables(positions, long_factor):
    half_rot = long_factor.shape[0]
    exponent = jnp.arange(half_rot, dtype=jnp.float32) / half_rot
    inv_freq = 1.0 / (long_factor * jnp.power(ROPE_BASE, exponent))
    angles = positions.astype(jnp.float32)[:, None] * inv_freq[None, :]
    return jnp.cos(angles) * ROPE_GAIN, jnp.sin(angles) * ROPE_GAIN


def rotate(head_vals, cos_t, sin_t, direction):
    half_rot = cos_t.shape[1]
    cos_b = cos_t[None, :, None, :]
    sin_b = sin_t[None, :, None, :] * direction
    first_half = head_vals[..., :half_rot]
    second_half = head_vals[..., half_rot:2 * half_rot]
    rest_dims = head_vals[..., 2 * half_rot:].astype(jnp.float32)
    return jnp.concatenate([first_half * cos_b - second_half * sin_b, second_half * cos_b + first_half * sin_b, rest_dims], axis=-1)


def norm_forward(hidden, norm_w):
    hidden_f = hidden.astype(jnp.float32)
    inv_rms = lax.rsqrt(jnp.mean(hidden_f * hidden_f, axis=-1, keepdims=True) + NORM_EPS)
    unit_rows = hidden_f * inv_rms
    return (unit_rows * norm_w.astype(jnp.float32)).astype(jnp.bfloat16), unit_rows, inv_rms


def norm_backward(grad_normed, unit_rows, inv_rms, norm_w):
    grad_unit = grad_normed * norm_w.astype(jnp.float32)
    mean_dot = jnp.mean(grad_unit * unit_rows, axis=-1, keepdims=True)
    return inv_rms * (grad_unit - unit_rows * mean_dot)


def split_fused(fused_qkv, n_heads, kv_heads, head_dim, cos_t, sin_t):
    n_batch, tok_len = fused_qkv.shape[0], fused_qkv.shape[1]
    q_width = n_heads * head_dim
    kv_width = kv_heads * head_dim
    queries = fused_qkv[..., :q_width].reshape(n_batch, tok_len, n_heads, head_dim)
    key_vals = fused_qkv[..., q_width:q_width + kv_width].reshape(n_batch, tok_len, kv_heads, head_dim)
    value_vals = fused_qkv[..., q_width + kv_width:].reshape(n_batch, tok_len, kv_heads, head_dim)
    return (rotate(queries, cos_t, sin_t, 1.0).astype(jnp.bfloat16), rotate(key_vals, cos_t, sin_t, 1.0).astype(jnp.bfloat16), value_vals.astype(jnp.bfloat16))


def merge_grads(grad_q, grad_k, grad_v, cos_t, sin_t):
    n_batch, tok_len = grad_q.shape[0], grad_q.shape[1]
    return jnp.concatenate([
        rotate(grad_q, cos_t, sin_t, -1.0).reshape(n_batch, tok_len, -1),
        rotate(grad_k, cos_t, sin_t, -1.0).reshape(n_batch, tok_len, -1),
        grad_v.astype(jnp.float32).reshape(n_batch, tok_len, -1)], axis=-1).astype(jnp.bfloat16)


def causal_probs(queries, key_vals):
    seq_len, head_dim = queries.shape[1], queries.shape[-1]
    scores = jnp.einsum('bqkge,bske->bkgqs', queries, key_vals, preferred_element_type=jnp.float32) * (head_dim ** -0.5)
    causal = jnp.arange(seq_len)[:, None] >= jnp.arange(seq_len)[None, :]
    return jax.nn.softmax(jnp.where(causal, scores, MASK_VALUE), axis=-1)


def attention_forward(queries, key_vals, value_vals):
    prob_mat = causal_probs(queries, key_vals)
    return jnp.einsum('bkgqs,bske->bqkge', prob_mat.astype(jnp.bfloat16), value_vals, preferred_element_type=jnp.float32).astype(jnp.bfloat16)


def attention_backward(queries, key_vals, value_vals, grad_attn):
    head_dim = queries.shape[-1]
    prob_mat = causal_probs(queries, key_vals)
    grad_v = jnp.einsum('bkgqs,bqkge->bske', prob_mat.astype(jnp.bfloat16), grad_attn, preferred_element_type=jnp.float32)
    grad_p = jnp.einsum('bqkge,bske->bkgqs', grad_attn, value_vals, preferred_element_type=jnp.float32)
    row_dot = jnp.sum(grad_p * prob_mat, axis=-1, keepdims=True)
    grad_s = (prob_mat * (grad_p - row_dot) * (head_dim ** -0.5)).astype(jnp.bfloat16)
    grad_q = jnp.einsum('bkgqs,bske->bqkge', grad_s, key_vals, preferred_element_type=jnp.float32)
    grad_k = jnp.einsum('bkgqs,bqkge->bske', grad_s, queries, preferred_element_type=jnp.float32)
    return grad_q.astype(jnp.bfloat16), grad_k.astype(jnp.bfloat16), grad_v.astype(jnp.bfloat16)


def solution(mesh):
    group_devs = mesh.shape['sp']
    to_heads = functools.partial(lax.all_to_all, axis_name='sp', split_axis=2, concat_axis=1, tiled=True)
    to_tokens = functools.partial(lax.all_to_all, axis_name='sp', split_axis=1, concat_axis=2, tiled=True)

    def device_step(hidden, norm_w, w_qkv, w_out, long_factor, grad_out):
        n_batch, tok_len = hidden.shape[0], hidden.shape[1]
        n_heads, head_dim = w_out.shape[0], w_out.shape[1]
        kv_heads = (w_qkv.shape[1] // head_dim - n_heads) // 2
        seq_len = tok_len * group_devs
        heads_local = n_heads // group_devs
        kv_local = kv_heads // group_devs
        head_shape = (n_batch, seq_len, kv_local, n_heads // kv_heads, head_dim)
        positions = lax.axis_index('sp') * tok_len + jnp.arange(tok_len)
        cos_t, sin_t = rope_tables(positions, long_factor)
        normed, unit_rows, inv_rms = norm_forward(hidden, norm_w)
        fused_qkv = jnp.einsum('btd,dw->btw', normed, w_qkv, preferred_element_type=jnp.float32)
        q_local, k_local, v_local = split_fused(fused_qkv, n_heads, kv_heads, head_dim, cos_t, sin_t)
        q_heads = to_heads(q_local).reshape(head_shape)
        k_heads = to_heads(k_local)
        v_heads = to_heads(v_local)
        attn_heads = attention_forward(q_heads, k_heads, v_heads)
        attn_local = to_tokens(attn_heads.reshape(n_batch, seq_len, heads_local, head_dim))
        projected = jnp.einsum('bthe,hed->btd', attn_local, w_out, preferred_element_type=jnp.float32)
        block_out = (hidden.astype(jnp.float32) + projected).astype(jnp.bfloat16)

        grad_w_out = jnp.einsum('bthe,btd->hed', attn_local, grad_out, preferred_element_type=jnp.float32)
        grad_attn = jnp.einsum('btd,hed->bthe', grad_out, w_out, preferred_element_type=jnp.float32).astype(jnp.bfloat16)
        grad_attn_heads = to_heads(grad_attn).reshape(head_shape)
        grad_q, grad_k, grad_v = attention_backward(q_heads, k_heads, v_heads, grad_attn_heads)
        grad_q_local = to_tokens(grad_q.reshape(n_batch, seq_len, heads_local, head_dim))
        grad_fused = merge_grads(grad_q_local, to_tokens(grad_k), to_tokens(grad_v), cos_t, sin_t)
        grad_w_qkv = jnp.einsum('btd,btw->dw', normed, grad_fused, preferred_element_type=jnp.float32)
        grad_normed = jnp.einsum('btw,dw->btd', grad_fused, w_qkv, preferred_element_type=jnp.float32)
        grad_hidden = (grad_out.astype(jnp.float32) + norm_backward(grad_normed, unit_rows, inv_rms, norm_w)).astype(jnp.bfloat16)
        grad_norm_w = jnp.sum(grad_normed * unit_rows, axis=(0, 1))
        return (block_out, grad_hidden, lax.psum(grad_w_qkv, 'sp'), lax.psum(grad_w_out, 'sp'), lax.psum(grad_norm_w, 'sp'))

    tok_spec = P('dp', 'sp', None)
    return jax.shard_map(device_step, mesh=mesh,
                         in_specs=(tok_spec, P(), P(), P(), P(), tok_spec),
                         out_specs=(tok_spec, tok_spec, P('dp', None), P('dp', None, None), P('dp')),
                         check_vma=False)
```

profile of v0, /device:TPU:0, one launch (start us, length us, event | category | flops | bytes accessed | tf_op | source)
XLA Modules:
  0.0 1349.5 jit_solution(17468303420598044489)
XLA Ops:
  11.6 17.1 %fusion.15 = f32[8,128,3072]{2,1,0:T(8,128)S(1)} fusion(bf16[2048,3072]{1,0:T(8,128)(2,1)} %param.8, bf16[8,128,2048]{2,1,0:T(8,128)(2,1)} %param.6, f32[2048]{0:T(1024)S(1)} %convert_element_type.108, f32[8,128]{1,0:T(8,128)S(1)} %add_rsqrt_fusion), kind=kOutput, calls=%fused_computation.20 | convolution fusion | flops 12893290496 | bytes 29372416 | tf_op jit(solution)/shard_map/btd,dw->btw/dot_general | solution.py:103
  28.8 4.8 copy-done.3
  39.3 4.3 all-to-all-start.1
  47.1 11.9 all-to-all-done.1
  61.2 7.9 slice.49
  69.1 9.1 copy.76
  78.2 4.7 subtract_convert_fusion
  84.2 3.4 copy.77
  87.7 3.5 all-to-all-start.2
  91.1 12.5 fusion.44
  106.6 33.6 %all-to-all-done.2 = bf16[8,128,32,64]{1,3,0,2:T(8,128)(2,1)} async-done(((bf16[8,128,32,64]{1,3,0,2:T(8,128)(2,1)}), bf16[8,128,32,64]{1,3,0,2:T(8,128)(2,1)}, u32[]{:S(2)}, u32[]{:S(2)}) %all-to-all-start.2) | async-done | bytes 4194336 | tf_op jit(solution)/shard_map/all_to_all | solution.py:105
  140.2 3.3 all-to-all-start.4
  150.2 12.7 copy.116
  163.0 7.5 reshape.201
  170.4 22.0 %all-to-all-done.4 = bf16[8,128,32,64]{1,3,0,2:T(8,128)(2,1)} async-done(((bf16[8,128,32,64]{1,3,0,2:T(8,128)(2,1)}), bf16[8,128,32,64]{1,3,0,2:T(8,128)(2,1)}, u32[]{:S(2)}, u32[]{:S(2)}) %all-to-all-start.4) | async-done | bytes 4194336 | tf_op jit(solution)/shard_map/all_to_all | solution.py:115
  192.4 12.3 copy.115
  204.8 7.3 reshape.204
  212.1 46.3 %fusion.6 = (f32[8,4,1024]{2,1,0:T(4,128)S(1)}, f32[8,1024,1024,4]{2,1,3,0:T(8,128)}) fusion(pred[1024,1024]{0,1:T(8,128)(4,1)S(1)} %iota_compare_fusion, bf16[8,1024,4,64]{1,3,2,0:T(8,128)(2,1)} %reshape.201, bf16[8,1024,64,1]{1,2,0,3:T(8,128)(2,1)S(1)} %reshape.210), kind=kOutput, calls=%fused_computation.10 | convolution fusion | flops 4395597824 | bytes 140640256 | tf_op jit(solution)/shard_map/bqkge,bske->bkgqs/dot_general | solution.py:65
  258.4 41.6 %fusion.5 = f32[8,4,1024]{2,1,0:T(4,128)S(1)} fusion(f32[8,1024,1024,4]{2,1,3,0:T(8,128)} %get-tuple-element.21, f32[8,4,1024]{2,1,0:T(4,128)S(1)} %get-tuple-element.20, pred[1024,1024]{0,1:T(8,128)(4,1)S(1)} %iota_compare_fusion), kind=kLoop, calls=%fused_computation.9 | loop fusion | flops 134184960 | bytes 135528448 | tf_op jit(solution)/shard_map/reduce_sum | solution.py:67
  300.0 99.7 %fusion = (f32[8,4,1024]{2,1,0:T(4,128)S(1)}, f32[8,1024,1024,4]{2,1,3,0:T(8,128)}) fusion(f32[8,4,1024]{2,1,0:T(4,128)S(1)} %fusion.5, f32[8,4,1024]{2,1,0:T(4,128)S(1)} %get-tuple-element.20, f32[8,1024,1024,4]{2,1,3,0:T(8,128)} %get-tuple-element.21, pred[1024,1024]{0,1:T(8,128)(4,1)S(1)} %iota_compare_fusion, bf16[8,1024,4,64]{1,3,2,0:T(8,128)(2,1)} %reshape.204, ...), kind=kOutput, calls=%fused_computation.3 | convolution fusion | flops 4496261120 | bytes 275120128 | tf_op jit(solution)/shard_map/bqkge,bske->bkgqs/dot_general | solution.py:79
  399.7 104.4 %fusion.7 = bf16[8,4,1024,1024]{2,3,1,0:T(8,128)(2,1)} fusion(f32[8,1024,1024,4]{2,1,3,0:T(8,128)} %get-tuple-element.23, f32[8,4,1024]{2,1,0:T(4,128)S(1)} %get-tuple-element.22, f32[8,4,1024]{2,1,0:T(4,128)S(1)} %fusion.5, f32[8,4,1024]{2,1,0:T(4,128)S(1)} %get-tuple-element.20, f32[8,1024,1024,4]{2,1,3,0:T(8,128)} %get-tuple-element.21, ...), kind=kLoop, calls=%fused_computation.11 | loop fusion | flops 268435456 | bytes 336986112 | tf_op jit(solution)/shard_map/reshape.30
  504.1 30.6 %fusion.53 = bf16[8,1024,1,64]{1,3,0,2:T(8,128)(2,1)} fusion(bf16[8,1024,4,64]{1,3,2,0:T(8,128)(2,1)} %reshape.201, bf16[8,4,1024,1024]{2,3,1,0:T(8,128)(2,1)} %fusion.7), kind=kOutput, calls=%fused_computation.67 | convolution fusion | flops 4295491584 | bytes 72351744 | tf_op jit(solution)/shard_map/bkgqs,bqkge->bske/dot_general | solution.py:83
  543.2 49.2 %fusion.54 = bf16[8,1024,1,64]{1,3,0,2:T(8,128)(2,1)} fusion(bf16[8,1024,4,64]{1,3,2,0:T(8,128)(2,1)} %reshape.204, f32[8,4,1024]{2,1,0:T(4,128)S(1)} %fusion.5, f32[8,4,1024]{2,1,0:T(4,128)S(1)} %get-tuple-element.20, f32[8,1024,1024,4]{2,1,3,0:T(8,128)} %get-tuple-element.21, pred[1024,1024]{0,1:T(8,128)(4,1)S(1)} %iota_compare_fusion), kind=kOutput, calls=%fused_computation.68 | convolution fusion | flops 4463263744 | bytes 140771328 | tf_op jit(solution)/shard_map/bkgqs,bqkge->bske/dot_general | solution.py:78
  600.6 25.8 %convert_bitcast_fusion = bf16[8,1024,4,64]{1,3,2,0:T(8,128)(2,1)} fusion(bf16[8,4,1024,1024]{2,3,1,0:T(8,128)(2,1)} %fusion.7, bf16[8,1024,64,1]{1,2,0,3:T(8,128)(2,1)} %copy-done.4), kind=kOutput, calls=%fused_computation.58 | convolution fusion | flops 4297064448 | bytes 72351744 | tf_op jit(solution)/shard_map/bkgqs,bske->bqkge/dot_general | solution.py:82
  626.4 13.6 %copy.85 = bf16[8,1024,4,64]{3,2,0,1:T(4,128)(2,1)} copy(bf16[8,1024,4,64]{1,3,2,0:T(8,128)(2,1)} %convert_bitcast_fusion) | data formatting | bytes 8388608 | tf_op jit(solution)/shard_map/reshape | solution.py:117
  640.0 10.6 reshape.227
  650.6 3.5 all-to-all-start.5
  654.1 49.7 %convert_bitcast_fusion.1 = bf16[8,1024,4,64]{1,3,2,0:T(8,128)(2,1)} fusion(bf16[8,1024,64,1]{1,2,0,3:T(8,128)(2,1)S(1)} %copy-done.10, f32[8,4,1024]{2,1,0:T(4,128)S(1)} %fusion.5, f32[8,4,1024]{2,1,0:T(4,128)S(1)} %get-tuple-element.20, f32[8,1024,1024,4]{2,1,3,0:T(8,128)} %get-tuple-element.21, pred[1024,1024]{0,1:T(8,128)(4,1)S(1)} %iota_compare_fusion), kind=kOutput, calls=%fused_computation.59 | convolution fusion | flops 4464836608 | bytes 140771328 | tf_op jit(solution)/shard_map/bkgqs,bske->bqkge/dot_general | solution.py:72
  703.8 13.6 %copy.80 = bf16[8,1024,4,64]{3,2,0,1:T(4,128)(2,1)} copy(bf16[8,1024,4,64]{1,3,2,0:T(8,128)(2,1)} %convert_bitcast_fusion.1) | data formatting | bytes 8388608 | tf_op jit(solution)/shard_map/reshape | solution.py:109
  717.4 10.5 reshape.221
  727.9 3.4 all-to-all-start.3
  731.4 3.4 reshape.226
  744.1 10.3 reshape.228
  754.4 12.3 copy.86
  766.7 3.8 fusion.35
  770.4 3.4 pad_maximum_fusion.2
  773.8 6.5 copy.95
  780.3 10.3 reshape.222
  790.6 12.3 copy.81
  802.9 14.1 %convolution_bitcast_fusion.1 = f32[32,64,2048]{2,1,0:T(8,128)} fusion(bf16[8,128,32,64]{1,3,2,0:T(8,128)(2,1)} %bitcast.206, bf16[8,128,2048]{2,1,0:T(8,128)(2,1)} %param.11), kind=kOutput, calls=%fused_computation.42 | convolution fusion | flops 8589934592 | bytes 25165824 | tf_op jit(solution)/shard_map/bthe,btd->hed/dot_general | solution.py:113
  817.1 18.3 %convolution_bitcast_fusion = f32[2048,3072]{1,0:T(8,128)} fusion(bf16[8,128,2048]{2,1,0:T(8,128)(2,1)S(1)} %copy-done.1, f32[2048]{0:T(1024)S(1)} %copy-done.16, f32[8,128]{1,0:T(8,128)S(1)} %copy-done.18, bf16[8,128,512]{2,1,0:T(8,128)(2,1)S(1)} %copy.97, bf16[8,128,512]{2,1,0:T(8,128)(2,1)S(1)} %copy-done.11, bf16[8,128,2048]{2,1,0:T(8,128)(2,1)S(1)} %copy-done.8), kind=kOutput, calls=%fused_computation.17 | convolution fusion | flops 12912164864 | bytes 35663872 | tf_op jit(solution)/shard_map/btd,btw->dw/dot_general | solution.py:119
  835.4 20.6 %fusion.27 = (f32[2048]{0:T(1024)S(1)}, f32[8,128]{1,0:T(8,128)S(1)}, f32[8,128,2048]{2,1,0:T(8,128)}) fusion(bf16[8,128,2048]{2,1,0:T(8,128)(2,1)} %param.6, f32[8,128]{1,0:T(8,128)S(1)} %copy-done.18, f32[2048]{0:T(1024)S(1)} %copy-done.16, bf16[2048,3072]{1,0:T(8,128)(2,1)} %param.8, bf16[8,128,512]{2,1,0:T(8,128)(2,1)S(1)} %copy.97, ...), kind=kOutput, calls=%fused_computation.35 | convolution fusion | flops 12918453248 | bytes 31481856 | tf_op jit(solution)/shard_map/btw,dw->btd/dot_general | solution.py:120
  856.0 24.4 %psum.23 = f32[2048]{0:T(1024)} all-reduce(f32[2048]{0:T(1024)S(1)} %get-tuple-element.5), channel_id=1, replica_groups=mesh['dp'=1,'sp'=8] {'sp'}, use_global_device_ids=true, to_apply=%region_8.9 | all-reduce | flops 2048 | bytes 16384 | tf_op jit(solution)/shard_map/psum | solution.py:123
  880.5 8.9 fusion.26
  890.3 12.8 fusion.29
  903.1 411.5 %all-reduce.3.cloned.1.call-done = (f32[2048,3072]{1,0:T(8,128)}, f32[32,64,2048]{2,1,0:T(8,128)}) async-done(((f32[2048,3072]{1,0:T(8,128)}, f32[32,64,2048]{2,1,0:T(8,128)}), (f32[2048,3072]{1,0:T(8,128)}, f32[32,64,2048]{2,1,0:T(8,128)})) %all-reduce.3.cloned.1.call-update) | async-done | bytes 41943056 | tf_op jit(solution)/shard_map/psum | solution.py:123
  1314.6 18.8 %copy.119 = f32[2048,3072]{1,0:T(8,128)} copy(f32[2048,3072]{1,0:T(8,128)} %get-tuple-element.27) | data formatting | bytes 50331648
  1336.3 6.2 copy.120
  (81 shorter events, 56.8 us)
Async XLA Ops:
  10.3 18.5 %copy-start.17 = (f32[8,128]{1,0:T(8,128)}, f32[8,128]{1,0:T(8,128)S(1)}, u32[]{:S(2)}) copy-start(f32[8,128]{1,0:T(8,128)S(1)} %add_rsqrt_fusion) | copy-start | bytes 12292
  11.0 17.8 %copy-start.15 = (f32[2048]{0:T(1024)}, f32[2048]{0:T(1024)S(1)}, u32[]{:S(2)}) copy-start(f32[2048]{0:T(1024)S(1)} %convert_element_type.108) | copy-start | bytes 24580
  28.8 4.8 copy-start.3
  37.8 40.5 %copy-start.12 = (f32[128,32]{0,1:T(8,128)}, f32[128,32]{0,1:T(8,128)S(1)}, u32[]{:S(2)}) copy-start(f32[128,32]{0,1:T(8,128)S(1)} %get-tuple-element.19) | copy-start | bytes 49156
  39.3 19.7 %all-to-all-start.1 = ((bf16[8,128,8,64]{1,3,0,2:T(8,128)(2,1)}), bf16[8,128,8,64]{1,3,0,2:T(8,128)(2,1)S(1)}, u32[]{:S(2)}, u32[]{:S(2)}) async-start(bf16[8,128,8,64]{1,3,0,2:T(8,128)(2,1)} %copy.74), calls=%async_computation.1 | async-start | bytes 2097152 | tf_op jit(solution)/shard_map/all_to_all | solution.py:106
  58.9 28.7 %all-to-all-start = ((bf16[8,128,8,64]{1,3,0,2:T(8,128)(2,1)}), bf16[8,128,8,64]{1,3,0,2:T(8,128)(2,1)S(1)}, u32[]{:S(2)}, u32[]{:S(2)}) async-start(bf16[8,128,8,64]{1,3,0,2:T(8,128)(2,1)} %copy.71), calls=%async_computation | async-start | bytes 2097152 | tf_op jit(solution)/shard_map/all_to_all | solution.py:107
  87.7 52.5 %all-to-all-start.2 = ((bf16[8,128,32,64]{1,3,0,2:T(8,128)(2,1)}), bf16[8,128,32,64]{1,3,0,2:T(8,128)(2,1)}, u32[]{:S(2)}, u32[]{:S(2)}) async-start(bf16[8,128,32,64]{1,3,0,2:T(8,128)(2,1)} %copy.77), calls=%async_computation.2 | async-start | bytes 8388608 | tf_op jit(solution)/shard_map/all_to_all | solution.py:105
  140.2 52.3 %all-to-all-start.4 = ((bf16[8,128,32,64]{1,3,0,2:T(8,128)(2,1)}), bf16[8,128,32,64]{1,3,0,2:T(8,128)(2,1)}, u32[]{:S(2)}, u32[]{:S(2)}) async-start(bf16[8,128,32,64]{1,3,0,2:T(8,128)(2,1)} %copy.82), calls=%async_computation.4 | async-start | bytes 8388608 | tf_op jit(solution)/shard_map/all_to_all | solution.py:115
  147.0 65.1 %copy-start.4 = (bf16[8,1024,64,1]{1,2,0,3:T(8,128)(2,1)}, bf16[8,1024,64,1]{1,2,0,3:T(8,128)(2,1)S(1)}, u32[]{:S(2)}) copy-start(bf16[8,1024,64,1]{1,2,0,3:T(8,128)(2,1)S(1)} %reshape.210) | copy-start | bytes 3145732
  150.2 149.8 %copy-start.9 = (bf16[8,1024,64,1]{1,2,0,3:T(8,128)(2,1)}, bf16[8,1024,64,1]{1,2,0,3:T(8,128)(2,1)S(1)}, u32[]{:S(2)}) copy-start(bf16[8,1024,64,1]{1,2,0,3:T(8,128)(2,1)S(1)} %reshape.211) | copy-start | bytes 3145732
  540.0 57.7 %all-to-all-start.6 = ((bf16[8,2,32768]{2,1,0:T(2,128)(2,1)}), bf16[8,2,32768]{2,1,0:T(2,128)(2,1)}, u32[]{:S(2)}, u32[]{:S(2)}) async-start(bf16[8,2,32768]{2,1,0:T(2,128)(2,1)} %reshape.225), calls=%async_computation.6 | async-start | bytes 2097152 | tf_op jit(solution)/shard_map/all_to_all | solution.py:118
  597.7 52.9 %all-to-all-start.7 = ((bf16[8,2,32768]{2,1,0:T(2,128)(2,1)}), bf16[8,2,32768]{2,1,0:T(2,128)(2,1)S(1)}, u32[]{:S(2)}, u32[]{:S(2)}) async-start(bf16[8,2,32768]{2,1,0:T(2,128)(2,1)} %reshape.223), calls=%async_computation.7 | async-start | bytes 2097152 | tf_op jit(solution)/shard_map/all_to_all | solution.py:118
  640.0 14.1 %copy-start.10 = (bf16[8,1024,64,1]{1,2,0,3:T(8,128)(2,1)S(1)}, bf16[8,1024,64,1]{1,2,0,3:T(8,128)(2,1)}, u32[]{:S(2)}) copy-start(bf16[8,1024,64,1]{1,2,0,3:T(8,128)(2,1)} %copy-done.9) | copy-start | bytes 3145732
  650.6 53.2 %copy-start.6 = (bf16[8,2,32768]{2,1,0:T(2,128)(2,1)}, bf16[8,2,32768]{2,1,0:T(2,128)(2,1)S(1)}, u32[]{:S(2)}) copy-start(bf16[8,2,32768]{2,1,0:T(2,128)(2,1)S(1)} %all-to-all-done.7) | copy-start | bytes 3145732
  650.6 77.3 %all-to-all-start.5 = ((bf16[8,2,131072]{2,1,0:T(2,128)(2,1)}), bf16[8,2,131072]{2,1,0:T(2,128)(2,1)}, u32[]{:S(2)}, u32[]{:S(2)}) async-start(bf16[8,2,131072]{2,1,0:T(2,128)(2,1)} %reshape.227), calls=%async_computation.5 | async-start | bytes 8388608 | tf_op jit(solution)/shard_map/all_to_all | solution.py:117
  727.9 9.2 copy-start.13
  727.9 9.2 copy-start.14
  727.9 52.5 %all-to-all-start.3 = ((bf16[8,2,131072]{2,1,0:T(2,128)(2,1)}), bf16[8,2,131072]{2,1,0:T(2,128)(2,1)}, u32[]{:S(2)}, u32[]{:S(2)}) async-start(bf16[8,2,131072]{2,1,0:T(2,128)(2,1)} %reshape.221), calls=%async_computation.3 | async-start | bytes 8388608 | tf_op jit(solution)/shard_map/all_to_all | solution.py:109
  731.3 8.8 copy-start.7
  731.3 583.2 %all-reduce.3.cloned.1.call-start = ((), (), s32[]{:S(2)}) async-start(), calls=%async_computation.8 | async-start | bytes 83886080 | tf_op jit(solution)/shard_map/psum | solution.py:123
  802.9 14.1 %copy-start.1 = (bf16[8,128,2048]{2,1,0:T(8,128)(2,1)S(1)}, bf16[8,128,2048]{2,1,0:T(8,128)(2,1)}, u32[]{:S(2)}) copy-start(bf16[8,128,2048]{2,1,0:T(8,128)(2,1)} %param.6) | copy-start | bytes 12582916
  802.9 14.1 %copy-start.8 = (bf16[8,128,2048]{2,1,0:T(8,128)(2,1)S(1)}, bf16[8,128,2048]{2,1,0:T(8,128)(2,1)}, u32[]{:S(2)}) copy-start(bf16[8,128,2048]{2,1,0:T(8,128)(2,1)} %copy.95) | copy-start | bytes 12582916
  802.9 14.1 %copy-start.11 = (bf16[8,128,512]{2,1,0:T(8,128)(2,1)S(1)}, bf16[8,128,512]{2,1,0:T(8,128)(2,1)}, u32[]{:S(2)}) copy-start(bf16[8,128,512]{2,1,0:T(8,128)(2,1)} %copy.96) | copy-start | bytes 3145732
  802.9 14.1 %copy-start.16 = (f32[2048]{0:T(1024)S(1)}, f32[2048]{0:T(1024)}, u32[]{:S(2)}) copy-start(f32[2048]{0:T(1024)} %copy-done.15) | copy-start | bytes 24580
  802.9 14.1 %copy-start.18 = (f32[8,128]{1,0:T(8,128)S(1)}, f32[8,128]{1,0:T(8,128)}, u32[]{:S(2)}) copy-start(f32[8,128]{1,0:T(8,128)} %copy-done.17) | copy-start | bytes 12292
  880.5 9.0 copy-start.2
  880.5 9.8 copy-start.5
  1314.6 21.8 %copy-start = (f32[32,64,2048]{2,1,0:T(8,128)S(1)}, f32[32,64,2048]{2,1,0:T(8,128)}, u32[]{:S(2)}) copy-start(f32[32,64,2048]{2,1,0:T(8,128)} %get-tuple-element.28) | copy-start | bytes 50331652
Sparse Core Ops, SparseCore 0:
  835.5 479.0 all-reduce.2
where the time goes:
time: 1360 us; the launch traced here: 1350 us
  waiting for transfers between devices  479 us (35%)
  matrix products  397 us (29%)
  local copies, waits for them, and re-layouts  233 us (17%)
  other arithmetic  176 us (13%)
  starting transfers between devices  26.4 us (2%)
  blocking collectives  24.4 us (2%)
  between operations  14.6 us (1%)
    psum x1, waiting for transfers between devices, device_step(): lax.psum(grad_w_qkv, 'sp')  411 us
    another operation x5, other arithmetic  115 us
    dot_general x1, matrix products, attention_backward(): jnp.einsum('bqkge,bske->bkgqs', grad_attn, value_vals, preferred_element_...  99.7 us
    unnamed x48, local copies, waits for them, and re-layouts  85.4 us
    dot_general x1, matrix products, attention_forward(): jnp.einsum('bkgqs,bske->bqkge', prob_mat.astype(jnp.bfloat16), value_vals...  49.7 us
    dot_general x1, matrix products, attention_backward(): jnp.einsum('bkgqs,bqkge->bske', prob_mat.astype(jnp.bfloat16), grad_attn,...  49.2 us
    dot_general x1, matrix products, causal_probs(): jnp.einsum('bqkge,bske->bkgqs', queries, key_vals, preferred_element_type...  46.3 us
    reduce_sum x1, other arithmetic, causal_probs(): return jax.nn.softmax(jnp.where(causal, scores, MASK_VALUE), axis=-1)  41.6 us
  transfers between devices with their start and end apart: 9, of which 4 were waited for; matrix products, arithmetic and copies ran while one was open for 25% of the time, Pallas kernels for 0%

commit v1 on v0

v1 whole, which is shorter than its diff:
```python
import functools
import math
import jax
import jax.numpy as jnp
from jax import lax
from jax.experimental import pallas as pl
from jax.experimental.pallas import tpu as pltpu
from jax.sharding import PartitionSpec as P

NORM_EPS = 1e-5
ROPE_BASE = 10000.0
ROPE_GAIN = math.sqrt(1.0 + math.log(32.0) / math.log(4096.0))
MASK_VALUE = -1e30
BLK = 256
LANES = 128
HEADS = 8
Q_COLS = 4 * LANES
PAIR_W = Q_COLS + 2 * LANES
K_COLS, V_COLS = pl.ds(Q_COLS, LANES), pl.ds(Q_COLS + LANES, LANES)
MESH = pl.DeviceIdType.MESH
VMEM_LIMIT = 67_000_000
COST_BYTES = 2**26
COST_FLOPS = 10**11


def rope_tables(seq_len, long_factor):
    half_rot = long_factor.shape[0]
    exponent = jnp.arange(half_rot, dtype=jnp.float32) / half_rot
    inv_freq = 1.0 / (long_factor * jnp.power(ROPE_BASE, exponent))
    angles = jnp.arange(seq_len, dtype=jnp.float32)[:, None] * inv_freq[None, :]
    cos_t, sin_t = jnp.cos(angles) * ROPE_GAIN, jnp.sin(angles) * ROPE_GAIN
    return (jnp.concatenate([cos_t, cos_t, cos_t, cos_t], axis=1),
            jnp.concatenate([-sin_t, sin_t, -sin_t, sin_t], axis=1))


def lane_rotate(vals, cos_v, sin_v):
    first = lax.broadcasted_iota(jnp.int32, vals.shape, 1) % 64 < 32
    partner = jnp.where(first, pltpu.roll(vals, LANES - 32, 1), pltpu.roll(vals, 32, 1))
    return vals * cos_v + partner * sin_v


def half_variants(vals, out_ref, rows):
    low = lax.broadcasted_iota(jnp.int32, vals.shape, 1) < 64
    swapped = pltpu.roll(vals, 64, 1)
    zero = jnp.zeros_like(vals)
    out_ref[0, rows, :] = jnp.where(low, vals, zero).astype(jnp.bfloat16)
    out_ref[1, rows, :] = jnp.where(low, zero, swapped).astype(jnp.bfloat16)
    out_ref[2, rows, :] = jnp.where(low, swapped, zero).astype(jnp.bfloat16)
    out_ref[3, rows, :] = jnp.where(low, zero, vals).astype(jnp.bfloat16)


def over_keys(reduce, vals):
    return reduce(vals, axis=0, keepdims=True)


def aligned(start, size):
    return pl.ds(pl.multiple_of(start, size), size)


def dot_nt(a, b):
    return lax.dot_general(a, b, (((1,), (1,)), ((), ())), preferred_element_type=jnp.float32)


def dot_nn(a, b):
    return lax.dot_general(a, b, (((1,), (0,)), ((), ())), preferred_element_type=jnp.float32)


def causal_diag(scores):
    keys = lax.broadcasted_iota(jnp.int32, scores.shape, 0)
    rows = lax.broadcasted_iota(jnp.int32, scores.shape, 1)
    return jnp.where(keys <= rows, scores, MASK_VALUE)


def load_weights(w_hbm, w_s, sem):
    width = w_hbm.shape[1]
    n_pairs = width // PAIR_W
    copies = []
    for pair in range(n_pairs):
        for src, dst, cols in ((pair * Q_COLS, 0, Q_COLS), (n_pairs * Q_COLS + pair * LANES, Q_COLS, LANES),
                               (width - (n_pairs - pair) * LANES, Q_COLS + LANES, LANES)):
            copies.append(pltpu.make_async_copy(w_hbm.at[:, pl.ds(src, cols)], w_s.at[:, pl.ds(pair * PAIR_W + dst, cols)], sem.at[len(copies)]))
    return copies


def greet_all(me, n_devs):
    barrier = pltpu.get_barrier_semaphore()
    for k in range(1, n_devs):
        pl.semaphore_signal(barrier, inc=1, device_id={'sp': lax.rem(me + k, n_devs)}, device_id_type=MESH)
    pl.semaphore_wait(barrier, n_devs - 1)


def enter_kernel(hidden, grad_out, gain_ref, w_hbm, x_out, gy_out, qkv_out, turned_out, x_s, own_s, w_s, h_s, turned_s, stage,
                 x_send, x_recv, gy_send, gy_recv, w_sem, out_sem, stage_sem):
    n_devs, tok, d_model = hidden.shape
    me = lax.axis_index('sp')

    def to_peer(src, dst, send_sem, recv_sem, k):
        peer = lax.rem(me + k, n_devs)
        return pltpu.make_async_remote_copy(src_ref=src.at[peer], dst_ref=dst.at[me], send_sem=send_sem.at[k], recv_sem=recv_sem.at[k],
                                            device_id={'sp': peer}, device_id_type=MESH)

    weights = load_weights(w_hbm, w_s, w_sem)
    own_x = pltpu.make_async_copy(hidden.at[me], x_s.at[me], x_send.at[0])
    own_in = pltpu.make_async_copy(grad_out.at[me], own_s, gy_send.at[0])
    own_out = pltpu.make_async_copy(own_s, gy_out.at[me], gy_recv.at[0])
    greet_all(me, n_devs)
    peers = range(1, n_devs)
    xs = [to_peer(hidden, x_s, x_send, x_recv, k) for k in peers]
    gys = [to_peer(grad_out, gy_out, gy_send, gy_recv, k) for k in peers]
    for copy in xs + gys + [own_x, own_in] + weights:
        copy.start()
    gain = gain_ref[...]

    def norm_block(block):
        def norm_rows(n, carry):
            rows = aligned(n * 16, 16)
            x_f = x_s[block, rows, :].astype(jnp.float32)
            inv_rms = lax.rsqrt(jnp.mean(x_f * x_f, axis=-1, keepdims=True) + NORM_EPS)
            h_s[block, rows, :] = (x_f * inv_rms * gain).astype(jnp.bfloat16)
            return carry
        lax.fori_loop(0, tok // 16, norm_rows, 0)

    own_x.wait()
    norm_block(me)
    for k, copy in zip(peers, xs):
        copy.wait()
        norm_block(lax.rem(me + n_devs - k, n_devs))
    own_in.wait()
    own_out.start()
    for copy in weights:
        copy.wait()
    keep_x = pltpu.make_async_copy(x_s, x_out, out_sem.at[0])
    keep_x.start()

    def keep_qkv(pair):
        return pltpu.make_async_copy(stage.at[pair % 2], qkv_out.at[:, pl.ds(pair * PAIR_W, PAIR_W)], stage_sem.at[pair % 2])

    half = n_devs // 2
    n_pairs = w_hbm.shape[1] // PAIR_W
    for pair in range(n_pairs):
        if pair > 1:
            keep_qkv(pair - 2).wait()

        def columns(n, carry):
            for m in range(2):
                left = h_s[pl.ds(m * half, half)].reshape(half * tok, d_model)
                stage[pair % 2, pl.ds(m * half * tok, half * tok), aligned(n * BLK, BLK)] = dot_nn(left, w_s[:, aligned(pair * PAIR_W + n * BLK, BLK)])
            return carry

        lax.fori_loop(0, PAIR_W // BLK, columns, 0)
        keep_qkv(pair).start()

    def turn(n, carry):
        cols = aligned(n * LANES, LANES)
        for block in range(n_devs):
            turned_s[cols, pl.ds(block * tok, tok)] = jnp.transpose(h_s[block, :, cols])
        return carry

    lax.fori_loop(0, d_model // LANES, turn, 0)
    keep_turned = pltpu.make_async_copy(turned_s, turned_out, out_sem.at[1])
    keep_turned.start()
    for copy in gys:
        copy.wait()
    for pair in range(n_pairs - 2, n_pairs):
        keep_qkv(pair).wait()
    keep_turned.wait()
    keep_x.wait()
    own_out.wait()


def enter(hidden, grad_out, gain, w_qkv):
    n_devs, tok, d_model = hidden.shape
    seq, width = n_devs * tok, w_qkv.shape[1]
    anywhere, vmem, dma = pl.BlockSpec(memory_space=pl.ANY), pltpu.VMEM, pltpu.SemaphoreType.DMA
    shape, bf16 = jax.ShapeDtypeStruct, jnp.bfloat16
    return pl.pallas_call(
        enter_kernel,
        in_specs=[anywhere, anywhere, pl.BlockSpec(memory_space=vmem), anywhere],
        out_specs=[anywhere] * 4,
        out_shape=[shape(hidden.shape, bf16), shape(hidden.shape, bf16), shape((seq, width), jnp.float32), shape((d_model, seq), bf16)],
        scratch_shapes=[vmem(hidden.shape, bf16), vmem((tok, d_model), bf16), vmem(w_qkv.shape, bf16), vmem(hidden.shape, bf16),
                        vmem((d_model, seq), bf16), vmem((2, seq, PAIR_W), jnp.float32)]
        + [dma((n_devs,))] * 4 + [dma((3 * width // PAIR_W,)), dma((2,)), dma((2,))],
        compiler_params=pltpu.CompilerParams(vmem_limit_bytes=VMEM_LIMIT, collective_id=2, has_side_effects=True),
        cost_estimate=pl.CostEstimate(flops=COST_FLOPS, bytes_accessed=COST_BYTES, transcendentals=COST_BYTES),
        name="enter",
    )(hidden, grad_out, gain, w_qkv)


def axis_bits():
    me = lax.axis_index('sp')
    coord = {1: lax.rem(me, 2), 2: lax.rem(lax.div(me, 2), 2), 4: lax.div(me, 4)}
    return coord, {bit: {'sp': me + bit * (1 - 2 * coord[bit])} for bit in (1, 2, 4)}


def entry_barrier(peers):
    barrier = pltpu.get_barrier_semaphore()
    for bit in (1, 2, 4):
        pl.semaphore_signal(barrier, inc=1, device_id=peers[bit], device_id_type=MESH)
    pl.semaphore_wait(barrier, 3)


ORDER_OF_HALF = ((2, 4), (4, 2))


def add_rows(dst_ref, a_ref, a_row, b_ref, b_row):
    def body(i, carry):
        step = pl.multiple_of(i * 16, 16)
        total = a_ref[aligned(a_row + step, 16), :] + b_ref[aligned(b_row + step, 16), :].astype(jnp.float32)
        dst_ref[pl.ds(step, 16), :] = total.astype(dst_ref.dtype)
        return carry
    lax.fori_loop(0, dst_ref.shape[0] // 16, body, 0)


class Reduce:
    def __init__(self, coord, peers, sent, own, total, scratch):
        self.coord, self.peers, self.sent, self.own, self.total = coord, peers, sent, own, total
        n = len(sent)
        self.recv_c, self.sum0, self.snd0, self.recv0, self.sum1, self.snd1, self.recv1 = (scratch[k * n:(k + 1) * n] for k in range(7))
        self.send_sem, self.recv_sem = scratch[7 * n:]
        self.n = n

    def copy(self, src, dst, sem, bit):
        return pltpu.make_async_remote_copy(src_ref=src, dst_ref=dst, send_sem=self.send_sem.at[sem], recv_sem=self.recv_sem.at[sem],
                                            device_id=self.peers[bit], device_id_type=MESH)

    def stage_c(self):
        return [self.copy(self.sent[t], self.recv_c[t], t, 1) for t in range(self.n)]

    def stage_s(self, k):
        snd, recv = (self.snd0, self.recv0) if k == 0 else (self.snd1, self.recv1)
        return [self.copy(snd[t].at[h], recv[t].at[h], self.n + 2 * self.n * k + 2 * t + h, ORDER_OF_HALF[h][k])
                for t in range(self.n) for h in range(2)]

    def start(self):
        for copy in self.stage_c():
            copy.start()

    def mid1(self):
        for copy in self.stage_c():
            copy.wait()
        for t in range(self.n):
            half = self.own[t].shape[0] // 2
            for h in range(2):
                c = self.coord[ORDER_OF_HALF[h][0]]
                row = h * half + (1 - c) * (half // 2)
                add_rows(self.snd0[t].at[h], self.own[t], row, self.recv_c[t], row)
        for copy in self.stage_s(0):
            copy.start()
        for t in range(self.n):
            half = self.own[t].shape[0] // 2
            for h in range(2):
                row = h * half + self.coord[ORDER_OF_HALF[h][0]] * (half // 2)
                add_rows(self.sum0[t].at[h], self.own[t], row, self.recv_c[t], row)

    def mid2(self):
        for copy in self.stage_s(0):
            copy.wait()
        for t in range(self.n):
            quarter = self.own[t].shape[0] // 4
            for h in range(2):
                row = (1 - self.coord[ORDER_OF_HALF[h][1]]) * (quarter // 2)
                add_rows(self.snd1[t].at[h], self.sum0[t].at[h], row, self.recv0[t].at[h], row)
        for copy in self.stage_s(1):
            copy.start()
        for t in range(self.n):
            quarter = self.own[t].shape[0] // 4
            for h in range(2):
                row = self.coord[ORDER_OF_HALF[h][1]] * (quarter // 2)
                add_rows(self.sum1[t].at[h], self.sum0[t].at[h], row, self.recv0[t].at[h], row)

    def end(self):
        for copy in self.stage_s(1):
            copy.wait()
        for t in range(self.n):
            for h in range(2):
                add_rows(self.total[t].at[h], self.sum1[t].at[h], 0, self.recv1[t].at[h], 0)

    @staticmethod
    def scratch_shapes(shapes):
        vmem = lambda dtype, div: [pltpu.VMEM((2, r // div, c) if div else (r, c), dtype) for r, c in shapes]
        n = len(shapes)
        return (vmem(jnp.bfloat16, 0) + vmem(jnp.float32, 4) + vmem(jnp.bfloat16, 4) + vmem(jnp.bfloat16, 4)
                + vmem(jnp.float32, 8) + vmem(jnp.bfloat16, 8) + vmem(jnp.bfloat16, 8)
                + [pltpu.SemaphoreType.DMA((5 * n,)), pltpu.SemaphoreType.DMA((5 * n,))])


class Gather:
    def __init__(self, peers, total, pieces, scratch):
        self.peers, self.total, self.pieces = peers, total, pieces
        self.send_sem, self.recv_sem, self.local_sem = scratch
        self.n = len(total)

    def copy(self, src, dst, sem, bit):
        return pltpu.make_async_remote_copy(src_ref=src, dst_ref=dst, send_sem=self.send_sem.at[sem], recv_sem=self.recv_sem.at[sem],
                                            device_id=self.peers[bit], device_id_type=MESH)

    def stage(self, k):
        copies = []
        for t in range(self.n):
            if k == 2:
                copies.append(self.copy(self.pieces[t].at[pl.ds(0, 8)], self.pieces[t].at[pl.ds(8, 8)], 4 * self.n + t, 1))
                continue
            for h in range(2):
                if k == 0:
                    src, dst = self.total[t].at[pl.ds(h, 1)], self.pieces[t].at[pl.ds(4 * h + 1, 1)]
                else:
                    src, dst = self.pieces[t].at[pl.ds(4 * h, 2)], self.pieces[t].at[pl.ds(4 * h + 2, 2)]
                copies.append(self.copy(src, dst, 2 * self.n * k + 2 * t + h, ORDER_OF_HALF[h][1 - k]))
        return copies

    def local(self):
        return [pltpu.make_async_copy(self.total[t].at[pl.ds(h, 1)], self.pieces[t].at[pl.ds(4 * h, 1)], self.local_sem.at[2 * t + h])
                for t in range(self.n) for h in range(2)]

    def start(self):
        for copy in self.stage(0) + self.local():
            copy.start()

    def mid1(self):
        for copy in self.stage(0) + self.local():
            copy.wait()
        for copy in self.stage(1):
            copy.start()

    def mid2(self):
        for copy in self.stage(1):
            copy.wait()
        for copy in self.stage(2):
            copy.start()

    def end(self):
        for copy in self.stage(2):
            copy.wait()

    @staticmethod
    def scratch_shapes(n):
        return [pltpu.SemaphoreType.DMA((5 * n,)), pltpu.SemaphoreType.DMA((5 * n,)), pltpu.SemaphoreType.DMA((2 * n,))]


def attn_kernel(qkv_ref, wo_ref, cos_ref, sin_ref, normed_ref, gy_ref,
                o_ref, out_ref, sent_q_out, sent_d_out, own_q_out, own_d_out, total_q_out, total_d_out, pieces_q, pieces_d, *scratch):
    scratch = list(scratch)
    take = lambda n: [scratch.pop(0) for _ in range(n)]
    q_s, do_s, k_var, v_var, k_t, v_t, ot_ref, dq_t, dk_acc, dv_acc = take(10)
    sent, own, total = take(2), take(2), take(2)
    pair = pl.program_id(0)
    coord, peers = axis_bits()
    reduce = Reduce(coord, peers, sent, own, total, take(16))
    gather = Gather(peers, total, [ref.at[jnp.maximum(pair - 2, 0)] for ref in (pieces_q, pieces_d)], take(3))
    turn_sem, out_sem = take(2)

    @pl.when(pair == 0)
    def _():
        entry_barrier(peers)

    @pl.when(pair > 0)
    def _():
        for n, bit in enumerate((1, 2, 4)):
            pl.semaphore_signal(turn_sem.at[n], inc=1, device_id=peers[bit], device_id_type=MESH)
        for n in range(3):
            pl.semaphore_wait(turn_sem.at[n], 1)
        reduce.start()

    @pl.when(pair > 1)
    def _():
        gather.start()

    def middle(first):
        @pl.when(pair > 0)
        def _():
            (reduce.mid1 if first else reduce.mid2)()

        @pl.when(pair > 1)
        def _():
            (gather.mid1 if first else gather.mid2)()

    seq = qkv_ref.shape[0]
    n_blk = seq // BLK

    def setup_block(i, carry):
        rows = aligned(i * LANES, LANES)
        cos_v, sin_v = cos_ref[rows, :], sin_ref[rows, :]
        for c in range(4):
            cols = pl.ds(c * LANES, LANES)
            q_s[c, rows, :] = (lane_rotate(qkv_ref[rows, cols], cos_v, sin_v) * 0.125).astype(jnp.bfloat16)
        k_rot = lane_rotate(qkv_ref[rows, K_COLS], cos_v, sin_v).astype(jnp.bfloat16).astype(jnp.float32)
        half_variants(k_rot, k_var, rows)
        k_t[:, rows] = jnp.transpose(k_rot).astype(jnp.bfloat16)
        v_val = qkv_ref[rows, V_COLS].astype(jnp.bfloat16).astype(jnp.float32)
        half_variants(v_val, v_var, rows)
        v_t[:, rows] = jnp.transpose(v_val).astype(jnp.bfloat16)
        return carry

    lax.fori_loop(0, seq // LANES, setup_block, 0)

    def grad_attn(n, carry):
        heads = aligned(n * 256, 256)
        for m in range(seq // 512):
            rows = pl.ds(m * 512, 512)
            block = dot_nt(gy_ref[rows, :], wo_ref[heads, :]).astype(jnp.bfloat16)
            do_s[2 * n, rows, :] = block[:, :LANES]
            do_s[2 * n + 1, rows, :] = block[:, LANES:]
        return carry

    lax.fori_loop(0, 2, grad_attn, 0)
    middle(True)
    dk_acc[...] = jnp.zeros_like(dk_acc)
    dv_acc[...] = jnp.zeros_like(dv_acc)
    half = lax.broadcasted_iota(jnp.int32, (BLK, LANES), 1) // 64

    def head_pair(hp, carry):
        kv = hp // 2
        sub_kv = pl.multiple_of(kv * 64, 64)
        for i in range(n_blk):
            rows = pl.ds(i * BLK, BLK)
            q_blk = q_s[hp, rows, :]
            do_blk = do_s[hp, rows, :]
            parts = [(pl.ds(i * BLK, BLK), True)]
            if i:
                parts.append((pl.ds(0, i * BLK), False))
            dv_sum, dk_sum = [0.0] * len(parts), [0.0] * len(parts)
            for par in range(2):
                var = kv * 2 + par
                sub_h = aligned(hp * LANES + par * 64, 64)
                q_mine = jnp.where(half == par, q_blk, jnp.zeros_like(q_blk))
                do_mine = jnp.where(half == par, do_blk, jnp.zeros_like(do_blk))
                scores, top = [], None
                for keys, is_diag in parts:
                    part = dot_nt(k_var[var, keys, :], q_blk)
                    if is_diag:
                        part = causal_diag(part)
                    scores.append(part)
                    part_top = over_keys(jnp.max, part)
                    top = part_top if top is None else jnp.maximum(top, part_top)
                exps = [jnp.exp(part - top) for part in scores]
                inv = 1.0 / sum(over_keys(jnp.sum, part) for part in exps)
                probs, grads, row_dot, attn = [], [], 0.0, 0.0
                for n, (keys, _) in enumerate(parts):
                    prob = exps[n] * inv
                    prob_b = prob.astype(jnp.bfloat16)
                    grad_p = dot_nt(v_var[var, keys, :], do_blk)
                    row_dot = row_dot + over_keys(jnp.sum, prob * grad_p)
                    attn = attn + dot_nn(v_t[pl.ds(sub_kv, 64), keys], prob_b)
                    dv_sum[n] = dv_sum[n] + dot_nn(prob_b, do_mine)
                    probs.append(prob)
                    grads.append(grad_p)
                ot_ref[sub_h, rows] = attn.astype(jnp.bfloat16)
                acc = 0.0
                for n, (keys, _) in enumerate(parts):
                    grad_s = (probs[n] * (grads[n] - row_dot)).astype(jnp.bfloat16)
                    dk_sum[n] = dk_sum[n] + dot_nn(grad_s, q_mine)
                    acc = acc + dot_nn(k_t[pl.ds(sub_kv, 64), keys], grad_s)
                dq_t[sub_h, rows] = acc
            for n, (keys, _) in enumerate(parts):
                dv_acc[kv, keys, :] += dv_sum[n]
                dk_acc[kv, keys, :] += dk_sum[n]
        return carry

    lax.fori_loop(0, HEADS // 2, head_pair, 0)

    def finish_block(i, carry):
        rows = aligned(i * LANES, LANES)
        cos_v, sin_v = cos_ref[rows, :], -sin_ref[rows, :]
        for c in range(4):
            cols = pl.ds(c * LANES, LANES)
            o_ref[rows, cols] = jnp.transpose(ot_ref[cols, rows])
            grad_q = jnp.transpose(dq_t[cols, rows]) * 0.125
            out_ref[rows, cols] = lane_rotate(grad_q, cos_v, sin_v).astype(jnp.bfloat16)
        low = lax.broadcasted_iota(jnp.int32, (LANES, LANES), 1) < 64
        merged = []
        for acc_ref in (dk_acc, dv_acc):
            first, second = acc_ref[0, rows, :], acc_ref[1, rows, :]
            merged.append(jnp.where(low, first + pltpu.roll(first, 64, 1), second + pltpu.roll(second, 64, 1)))
        out_ref[rows, K_COLS] = lane_rotate(merged[0], cos_v, sin_v).astype(jnp.bfloat16)
        out_ref[rows, V_COLS] = merged[1].astype(jnp.bfloat16)
        return carry

    lax.fori_loop(0, seq // LANES, finish_block, 0)
    mine = coord[1]
    rows_q, rows_d = own[0].shape[0], own[1].shape[0]

    def weight_q(n, carry):
        cols = aligned(n * 256, 256)
        for m in range(rows_q // 512):
            rows = pl.ds(m * 512, 512)
            for half, ref in ((1 - mine, sent[0]), (mine, own[0])):
                left = normed_ref[aligned(half * rows_q + m * 512, 512), :]
                ref[rows, cols] = dot_nn(left, out_ref[:, cols]).astype(ref.dtype)
        return carry

    def weight_d(n, carry):
        cols = aligned(n * 256, 256)
        for half, ref in ((1 - mine, sent[1]), (mine, own[1])):
            left = ot_ref[aligned(half * rows_d, rows_d), :]
            ref[:, cols] = dot_nn(left, gy_ref[:, cols]).astype(ref.dtype)
        return carry

    middle(False)
    lax.fori_loop(0, PAIR_W // 256, weight_q, 0)
    lax.fori_loop(0, gy_ref.shape[1] // 256, weight_d, 0)

    @pl.when(pair > 0)
    def _():
        reduce.end()

    @pl.when(pair > 1)
    def _():
        gather.end()

    @pl.when(pair == pl.num_programs(0) - 1)
    def _():
        outs = [sent_q_out, sent_d_out, own_q_out, own_d_out, total_q_out, total_d_out]
        copies = [pltpu.make_async_copy(src, dst, out_sem.at[n]) for n, (src, dst) in enumerate(zip(sent + own + total, outs))]
        for copy in copies:
            copy.start()
        for copy in copies:
            copy.wait()


def total_shapes(own):
    return [jax.ShapeDtypeStruct((2, o.shape[0] // 8, o.shape[1]), jnp.bfloat16) for o in own]


def piece_shapes(total):
    return [jax.ShapeDtypeStruct((16,) + t.shape[1:], jnp.bfloat16) for t in total]


def attention(qkv, w_o, cos_t, sin_t, normed_t, grad_y):
    seq, d_model = grad_y.shape
    n_pairs = qkv.shape[1] // PAIR_W
    q_cols = HEADS * 64
    const = lambda shape: pl.BlockSpec(shape, lambda p: (0,) * len(shape), pipeline_mode=pl.Buffered(1))
    col = lambda width: pl.BlockSpec((seq, width), lambda p: (0, p))
    anywhere = pl.BlockSpec(memory_space=pl.ANY)
    shape = jax.ShapeDtypeStruct
    slab = pltpu.VMEM((4, seq, LANES), jnp.bfloat16)
    turned = pltpu.VMEM((LANES, seq), jnp.bfloat16)
    acc = pltpu.VMEM((2, seq, LANES), jnp.float32)
    partial = [(d_model // 2, PAIR_W), (q_cols // 2, d_model)]
    own = [shape(p, jnp.float32) for p in partial]
    sent = [shape(p, jnp.bfloat16) for p in partial]
    totals = total_shapes(own)
    pieces = [shape((n_pairs - 2,) + p.shape, p.dtype) for p in piece_shapes(totals)]
    kept = [pltpu.VMEM(p.shape, p.dtype) for p in sent + own + totals]
    out = pl.pallas_call(
        attn_kernel,
        grid=(n_pairs,),
        in_specs=[col(PAIR_W), pl.BlockSpec((q_cols, d_model), lambda p: (p, 0)), const((seq, LANES)), const((seq, LANES)), const((d_model, seq)), const((seq, d_model))],
        out_specs=[col(q_cols), col(PAIR_W)] + [anywhere] * 8,
        out_shape=[shape((seq, q_cols * n_pairs), jnp.bfloat16), shape((seq, PAIR_W * n_pairs), jnp.bfloat16)] + sent + own + totals + pieces,
        scratch_shapes=[slab, slab, slab, slab, turned, turned, pltpu.VMEM((q_cols, seq), jnp.bfloat16), pltpu.VMEM((q_cols, seq), jnp.float32), acc, acc]
        + kept + Reduce.scratch_shapes(partial) + Gather.scratch_shapes(2)
        + [pltpu.SemaphoreType.REGULAR((3,)), pltpu.SemaphoreType.DMA((6,))],
        compiler_params=pltpu.CompilerParams(vmem_limit_bytes=VMEM_LIMIT, collective_id=0, has_side_effects=True),
        cost_estimate=pl.CostEstimate(flops=COST_FLOPS, bytes_accessed=COST_BYTES, transcendentals=COST_BYTES),
        name="attn",
    )(qkv, w_o, cos_t, sin_t, normed_t, grad_y)
    return out[0], out[1], (list(out[2:4]), list(out[4:6])), list(out[6:8]), out[8:10]


def finish_kernel(o_ref, x_ref, grads_ref, gy_ref, gain_ref, wo_ref, w_hbm, sent_q, sent_d, own_q, own_d, old_q, old_d,
                  y_out, gh_out, old_pieces_q, old_pieces_d, pieces_q, pieces_d, norm_out, *scratch):
    scratch = list(scratch)
    take = lambda n: [scratch.pop(0) for _ in range(n)]
    y_s, gh_s, w_s, dh_s, norm_ref, norm_row, norm_all = take(7)
    total = take(2)
    step = pl.program_id(0)
    me = lax.axis_index('sp')
    coord, peers = axis_bits()
    reduce = Reduce(coord, peers, [sent_q, sent_d], [own_q, own_d], total, take(16))
    gather = Gather(peers, [old_q, old_d], [old_pieces_q, old_pieces_d], take(3))
    last = Gather(peers, total, [pieces_q, pieces_d], take(3))
    w_sem, y_send, y_recv, gh_send, gh_recv, norm_send, norm_recv = take(7)
    n_devs = y_out.shape[0]
    tok = y_out.shape[1]
    half_steps = pl.num_programs(0) // 2
    per_step = n_devs // half_steps
    weights = load_weights(w_hbm, w_s, w_sem)

    def share(values, out, send_sem, recv_sem, dest, act):
        @pl.when(dest == me)
        def _():
            act(pltpu.make_async_copy(values.at[dest], out.at[dest], send_sem.at[dest]), True)

        @pl.when(dest != me)
        def _():
            act(pltpu.make_async_remote_copy(src_ref=values.at[dest], dst_ref=out.at[me], send_sem=send_sem.at[dest], recv_sem=recv_sem.at[me],
                                             device_id={'sp': dest}, device_id_type=MESH), False)

    def send(values, out, send_sem, recv_sem, dests):
        for dest in dests:
            share(values, out, send_sem, recv_sem, dest, lambda copy, local: copy.start())

    def finish(values, out, send_sem, recv_sem):
        for peer in range(n_devs):
            @pl.when(peer == me)
            def _():
                pltpu.make_async_copy(values.at[peer], out.at[peer], send_sem.at[peer]).wait()

            @pl.when(peer != me)
            def _():
                pltpu.make_async_remote_copy(src_ref=values.at[peer], dst_ref=out.at[peer], send_sem=send_sem.at[peer], recv_sem=recv_sem.at[peer],
                                             device_id={'sp': peer}, device_id_type=MESH).wait()

    def share_norm(act):
        for k in range(1, n_devs):
            peer = lax.rem(me + k, n_devs)
            copy = pltpu.make_async_remote_copy(src_ref=norm_row, dst_ref=norm_all.at[me], send_sem=norm_send.at[k], recv_sem=norm_recv.at[k],
                                                device_id={'sp': peer}, device_id_type=MESH)
            act(copy)

    @pl.when(step == 0)
    def _():
        greet_all(me, n_devs)
        reduce.start()
        gather.start()
        for copy in weights:
            copy.start()
        norm_ref[...] = jnp.zeros_like(norm_ref)

    @pl.when(step == 1)
    def _():
        reduce.mid1()
        gather.mid1()

    @pl.when(jnp.logical_and(step >= 1, step <= half_steps))
    def _():
        send(y_s, y_out, y_send, y_recv, [(step - 1) * per_step + k for k in range(per_step)])

    d_model = wo_ref.shape[1]

    @pl.when(step < half_steps)
    def _():
        def cols_of_y(n, carry):
            cols = aligned(n * 512, 512)
            block = (x_ref[:, cols].astype(jnp.float32) + dot_nn(o_ref[...], wo_ref[:, cols])).astype(jnp.bfloat16)
            for k in range(per_step):
                y_s[step * per_step + k, :, cols] = block[k * tok:(k + 1) * tok, :]
            return carry
        lax.fori_loop(0, d_model // 512, cols_of_y, 0)

    @pl.when(step == half_steps)
    def _():
        for copy in weights:
            copy.wait()

    @pl.when(step >= half_steps)
    def _():
        def cols_of_dh(n, carry):
            rows = aligned(n * 512, 512)
            dh_s[:, rows] = dot_nt(grads_ref[...], w_s[rows, :])
            return carry
        lax.fori_loop(0, d_model // 512, cols_of_dh, 0)
        gain = gain_ref[...]

        def norm_rows(n, carry):
            rows = aligned(n * 16, 16)
            x_f = x_ref[rows, :].astype(jnp.float32)
            inv_rms = lax.rsqrt(jnp.mean(x_f * x_f, axis=-1, keepdims=True) + NORM_EPS)
            unit = x_f * inv_rms
            grad_normed = dh_s[rows, :]
            grad_unit = grad_normed * gain
            mean_dot = jnp.mean(grad_unit * unit, axis=-1, keepdims=True)
            grad_x = gy_ref[rows, :].astype(jnp.float32) + inv_rms * (grad_unit - unit * mean_dot)
            place = (step - half_steps) * per_step + n // (tok // 16)
            gh_s[place, aligned(lax.rem(n, tok // 16) * 16, 16), :] = grad_x.astype(jnp.bfloat16)
            weighted = grad_normed * unit
            norm_ref[...] += weighted[:8, :] + weighted[8:, :]
            return carry
        lax.fori_loop(0, per_step * tok // 16, norm_rows, 0)

    @pl.when(step == pl.num_programs(0) - 1)
    def _():
        gh = (gh_s, gh_out, gh_send, gh_recv)
        norm_row[...] = over_keys(jnp.sum, norm_ref[...])
        reduce.mid2()
        gather.mid2()
        share_norm(lambda copy: copy.start())
        send(*gh, range(n_devs // 2))
        reduce.end()
        last.start()
        send(*gh, range(n_devs // 2, n_devs))
        gather.end()
        last.mid1()
        last.mid2()
        share_norm(lambda copy: copy.wait())
        norm_all[me] = norm_row[...]
        norm_out[...] = sum(norm_all[peer] for peer in range(n_devs))
        finish(y_s, y_out, y_send, y_recv)
        last.end()
        finish(*gh)


def finish(attn, x, grads, grad_y, gain, w_o, w_qkv, reduce, old_total, n_devs):
    seq, d_model = x.shape
    sent, own = reduce
    steps = 8
    rows = 2 * seq // steps
    tok = seq // n_devs
    const = lambda shape: pl.BlockSpec(shape, lambda s: (0,) * len(shape), pipeline_mode=pl.Buffered(1))
    early = lambda width: pl.BlockSpec((rows, width), lambda s: (jnp.minimum(s, steps // 2 - 1), 0))
    late = lambda width: pl.BlockSpec((rows, width), lambda s: (jnp.maximum(s - steps // 2, 0), 0))
    anywhere = pl.BlockSpec(memory_space=pl.ANY)
    shape = jax.ShapeDtypeStruct
    totals = total_shapes(own)
    tokens = shape((n_devs, tok, d_model), jnp.bfloat16)
    dma = lambda: pltpu.SemaphoreType.DMA((n_devs,))
    out = pl.pallas_call(
        finish_kernel,
        grid=(steps,),
        in_specs=[early(q_w) for q_w in (attn.shape[1],)] + [pl.BlockSpec((rows, d_model), lambda s: (lax.rem(s, steps // 2), 0)), late(grads.shape[1]), late(d_model),
                  const((1, d_model)), const(w_o.shape), anywhere, anywhere, anywhere]
        + [const(o.shape) for o in own] + [const(t.shape) for t in totals],
        out_specs=[anywhere] * 6 + [pl.BlockSpec((1, d_model), lambda s: (0, 0))],
        out_shape=[tokens, tokens] + piece_shapes(totals) + piece_shapes(totals) + [shape((1, d_model), jnp.float32)],
        scratch_shapes=[pltpu.VMEM(tokens.shape, jnp.bfloat16), pltpu.VMEM(tokens.shape, jnp.bfloat16),
                        pltpu.VMEM(w_qkv.shape, jnp.bfloat16), pltpu.VMEM((rows, d_model), jnp.float32),
                        pltpu.VMEM((8, d_model), jnp.float32), pltpu.VMEM((1, d_model), jnp.float32),
                        pltpu.VMEM((n_devs, 1, d_model), jnp.float32)]
        + [pltpu.VMEM(t.shape, t.dtype) for t in totals]
        + Reduce.scratch_shapes([o.shape for o in own]) + Gather.scratch_shapes(2) + Gather.scratch_shapes(2)
        + [pltpu.SemaphoreType.DMA((3 * w_qkv.shape[1] // PAIR_W,))] + [dma()] * 6,
        compiler_params=pltpu.CompilerParams(vmem_limit_bytes=VMEM_LIMIT, collective_id=1, has_side_effects=True),
        cost_estimate=pl.CostEstimate(flops=COST_FLOPS, bytes_accessed=COST_BYTES, transcendentals=COST_BYTES),
        name="finish",
    )(attn, x, grads, grad_y, gain, w_o, w_qkv, *sent, *own, *old_total)
    return out[0], out[1], out[2:4], out[4:6], out[6]


def place_kernel(n_pairs, slots, *refs):
    pieces_q, pieces_d, tokens = refs[:n_pairs], refs[n_pairs:2 * n_pairs], refs[2 * n_pairs:2 * n_pairs + 2]
    q_out, d_out, *tokens_out = refs[2 * n_pairs + 2:]
    for src, dst in zip(tokens, tokens_out):
        dst[...] = src[...]
    for pair in range(n_pairs):
        d_out[pair] = pieces_d[pair][0, 0].astype(jnp.float32)
        for src, dst, width in ((0, pair * 512, 512), (512, n_pairs * 512 + pair * LANES, LANES),
                                (640, n_pairs * 640 + pair * LANES, LANES)):
            q_out[:, dst:dst + width] = pieces_q[pair][0, 0, :, src:src + width].astype(jnp.float32)


def place(slots, parts_q, parts_d, tokens):
    specs, args, sizes = [], [], []
    for parts in (parts_q, parts_d):
        chunks = [(part, c) for part in parts for c in range(part.shape[0])]
        rows, width = parts[0].shape[2:]
        specs += [pl.BlockSpec((1, 1, rows, width), lambda s, slots, c=c: (c, s, 0, 0)) for _, c in chunks]
        args += [part for part, _ in chunks]
        sizes.append((len(chunks), rows, width))
    (n_pairs, rows_q, width_q), (_, rows_d, width_d) = sizes
    flat = [t.reshape(16, -1, t.shape[-1]) for t in tokens]
    through = pl.BlockSpec((1,) + flat[0].shape[1:], lambda s, slots: (s, 0, 0))
    shape = jax.ShapeDtypeStruct
    grad_q, grad_d, *out = pl.pallas_call(
        functools.partial(place_kernel, n_pairs),
        grid_spec=pltpu.PrefetchScalarGridSpec(
            num_scalar_prefetch=1, grid=(16,), in_specs=specs + [through] * 2,
            out_specs=[pl.BlockSpec((rows_q, n_pairs * width_q), lambda s, slots: (slots[s], 0)),
                       pl.BlockSpec((n_pairs, rows_d, width_d), lambda s, slots: (0, slots[s], 0)), through, through]),
        out_shape=[shape((16 * rows_q, n_pairs * width_q), jnp.float32), shape((n_pairs, 16 * rows_d, width_d), jnp.float32)]
        + [shape(t.shape, t.dtype) for t in flat],
        compiler_params=pltpu.CompilerParams(vmem_limit_bytes=VMEM_LIMIT),
        cost_estimate=pl.CostEstimate(flops=COST_FLOPS, bytes_accessed=COST_BYTES, transcendentals=COST_BYTES),
        name="place",
    )(slots, *args, *flat)
    return grad_q, grad_d, [o.reshape(t.shape) for o, t in zip(out, tokens)]


def row_slots():
    me = lax.axis_index('sp')
    core, x, y = me & 1, (me >> 1) & 1, me >> 2
    order = []
    for c in (core, 1 - core):
        for half, (a, b) in enumerate(((x, y), (y, x))):
            for a_i in (a, 1 - a):
                for b_i in (b, 1 - b):
                    order.append(c * 8 + half * 4 + a_i * 2 + b_i)
    return jnp.stack(order).astype(jnp.int32)


def solution(mesh):
    n_devs = mesh.shape['sp']

    def device_step(hidden, norm_w, w_qkv, w_out, long_factor, grad_out):
        d_model = hidden.shape[-1]
        gain = norm_w.astype(jnp.float32)[None]
        x, grad_y, qkv, normed_t = enter(hidden, grad_out, gain, w_qkv)
        x, grad_y = x.reshape(-1, d_model), grad_y.reshape(-1, d_model)
        cos_t, sin_t = rope_tables(len(x), long_factor)
        w_o = w_out.reshape(-1, d_model)
        attn, grads, partial, total, pieces = attention(qkv, w_o, cos_t, sin_t, normed_t, grad_y)
        block_out, grad_hidden, before_last, last, grad_norm_w = finish(attn, x, grads, grad_y, gain, w_o, w_qkv, partial, total, n_devs)
        parts = [[first, second[None], third[None]] for first, second, third in zip(pieces, before_last, last)]
        grad_w_qkv, grad_w_out, (block_out, grad_hidden) = place(row_slots(), *parts, (block_out, grad_hidden))
        return block_out, grad_hidden, grad_w_qkv, grad_w_out.reshape(w_out.shape), grad_norm_w.reshape(-1)

    tok_spec = P('dp', 'sp', None)
    return jax.shard_map(device_step, mesh=mesh,
                         in_specs=(tok_spec, P(), P(), P(), P(), tok_spec),
                         out_specs=(tok_spec, tok_spec, P('dp', None), P('dp', None, None), P('dp')),
                         check_vma=False)
```

time: 1360 us -> 508 us (0.37)
  Pallas kernels: 0 us -> 500 us
  waiting for transfers between devices: 479 us -> 0 us
  matrix products: 397 us -> 0 us
  local copies, waits for them, and re-layouts: 233 us -> 1.3 us
  other arithmetic: 176 us -> 5.8 us
  starting transfers between devices: 26.4 us -> 0 us
  blocking collectives: 24.4 us -> 0 us
  between operations: 14.6 us -> 0.71 us
    pallas_call x0 -> x4, Pallas kernels: none -> 500 us  [the longest x1 203 us: attention(): pl.pallas_call(attn_kernel, grid=(n_pairs,), in_specs=[col(PAIR_W), pl.Bl...]
    psum x1 -> x0, waiting for transfers between devices: 411 us -> none  [device_step(): lax.psum(grad_w_qkv, 'sp')]
    dot_general x12 -> x0, matrix products: 397 us -> none  [the longest x1 99.7 us: attention_backward(): jnp.einsum('bqkge,bske->bkgqs', grad_attn, value_vals, preferred_element_...]
    another operation x5 -> x0, other arithmetic: 115 us -> none
    unnamed x48 -> x3, local copies, waits for them, and re-layouts: 85.4 us -> 0.61 us
    all_to_all x8 -> x0, waiting for transfers between devices: 67.5 us -> none  [the longest x1 33.6 us: device_step(): q_heads = to_heads(q_local).reshape(head_shape)]
    all_to_all x7 -> x0, local copies, waits for them, and re-layouts: 55.3 us -> none  [the longest x1 12.7 us: device_step(): q_heads = to_heads(q_local).reshape(head_shape)]
    reduce_sum x2 -> x0, other arithmetic: 44.7 us -> none  [the longest x1 41.6 us: causal_probs(): return jax.nn.softmax(jnp.where(causal, scores, MASK_VALUE), axis=-1)]
  transfers between devices with their start and end apart: 9 -> 0, of which waited for: 4 -> 0; matrix products, arithmetic and copies ran while one was open for 25% -> 0% of each run, Pallas kernels for 0% -> 0%
where the time goes in v1:
time: 508 us
  Pallas kernels  500 us (98%)
  other arithmetic  5.8 us (1%)
    pallas_call x1, Pallas kernels, attention(): pl.pallas_call(attn_kernel, grid=(n_pairs,), in_specs=[col(PAIR_W), pl.Bl...  203 us
    pallas_call x1, Pallas kernels, finish(): pl.pallas_call(finish_kernel, grid=(steps,), in_specs=[early(q_w) for q_w...  172 us
    pallas_call x1, Pallas kernels, enter(): pl.pallas_call(enter_kernel, in_specs=[anywhere, anywhere, pl.BlockSpec(m...  96.1 us
    pallas_call x1, Pallas kernels, place(): pl.pallas_call(functools.partial(place_kernel, n_pairs), grid_spec=pltpu....  29.1 us

profile of v1, /device:TPU:0, one launch (start us, length us, event | category | flops | bytes accessed | tf_op | source)
XLA Modules:
  0.0 507.6 jit_solution(10335751839437809439)
XLA Ops:
  0.7 0.7 stack.67.slots
  1.4 0.7 multiply_divide_fusion
  2.0 1.3 broadcast_in_dim.25
  3.3 2.0 fusion
  5.3 1.8 pad_maximum_fusion
  7.2 96.1 %enter.1 = (bf16[8,128,2048]{2,1,0:T(8,128)(2,1)}, bf16[8,128,2048]{2,1,0:T(8,128)(2,1)}, f32[1024,3072]{1,0:T(8,128)}, bf16[2048,1024]{1,0:T(8,128)(2,1)}) custom-call(bf16[8,128,2048]{2,1,0:T(8,128)(2,1)} %hidden.1, bf16[8,128,2048]{2,1,0:T(8,128)(2,1)} %grad_out.1, f32[1,2048]{1,0:T(1,128)} %bitcast.30, bf16[2048,3072]{1,0:T(8,128)(2,1)} %w_hbm.3), custom_call_target="tpu_custom_call" | custom-call | flops 99999997952 | bytes 67108864 | tf_op jit(solution)/shard_map/enter/pallas_call | solution.py:176
  103.3 202.8 %attn.1 = (bf16[1024,2048]{1,0:T(8,128)(2,1)}, bf16[1024,3072]{1,0:T(8,128)(2,1)}, bf16[1024,768]{1,0:T(8,128)(2,1)}, bf16[256,2048]{1,0:T(8,128)(2,1)}, f32[102...) custom-call(f32[1024,3072]{1,0:T(8,128)} %get-tuple-element.30.qkv_r, ...), custom_call_target="tpu_custom_call" | custom-call | flops 99999997952 | bytes 67108864 | tf_op jit(solution)/shard_map/attn/pallas_call | solution.py:546
  306.1 171.8 %finish.1 = (bf16[8,128,2048]{2,1,0:T(8,128)(2,1)}, bf16[8,128,2048]{2,1,0:T(8,128)(2,1)}, bf16[16,128,768]{2,1,0:T(8,128)(2,1)}, bf16[16,32,2048]{2,1,0:T(8,128...) custom-call(bf16[1024,2048]{1,0:T(8,128)(2,1)} %get-tuple-element.34.o_ref, ...), custom_call_target="tpu_custom_call" | custom-call | flops 99999997952 | bytes 67108864 | tf_op jit(solution)/shard_map/finish/pallas_call | solution.py:709
  477.9 0.0 copy-start
  477.9 29.1 %place.1 = (f32[2048,3072]{1,0:T(8,128)}, f32[4,512,2048]{2,1,0:T(8,128)}, bf16[16,64,2048]{2,1,0:T(8,128)(2,1)}, bf16[16,64,2048]{2,1,0:T(8,128)(2,1)}) custom-call(s32[16]{0:T(128)} %stack.67.slots, bf16[2,16,128,768]{3,2,1,0:T(8,128)(2,1)} %get-tuple-element.33.refs_0_.refs_1_, bf16[2,16,128,768]{3,2,1,0:T(8,128)(2,1)} %get-tuple-element.33.refs_0_.refs_1_, ...), custom_call_target="tpu_custom_call" | custom-call | flops 99999997952 | bytes 67108864 | tf_op jit(solution)/shard_map/place/pallas_call | solution.py:755
  507.0 0.0 copy-done
  507.0 0.6 copy.13
Async XLA Ops:
  477.9 29.1 %copy-start = (f32[1,2048]{1,0:T(1,128)S(1)}, f32[1,2048]{1,0:T(1,128)}, u32[]{:S(2)}) copy-start(f32[1,2048]{1,0:T(1,128)} %get-tuple-element.54) | copy-start | bytes 24580

commit v2 on v1

--- a/solution.py
+++ b/solution.py
@@ -12,41 +12,52 @@
 ROPE_GAIN = math.sqrt(1.0 + math.log(32.0) / math.log(4096.0))
 MASK_VALUE = -1e30
 BLK = 256
+TALL = 512
 LANES = 128
-HEADS = 8
-Q_COLS = 4 * LANES
-PAIR_W = Q_COLS + 2 * LANES
-K_COLS, V_COLS = pl.ds(Q_COLS, LANES), pl.ds(Q_COLS + LANES, LANES)
+HEAD = LANES // 2
+Q_COLS = 2 * LANES
+GROUP_W = Q_COLS + LANES
+PAIR_W = 2 * GROUP_W
+KV_COLS = pl.ds(Q_COLS, LANES)
 MESH = pl.DeviceIdType.MESH
 VMEM_LIMIT = 67_000_000
 COST_BYTES = 2**26
 COST_FLOPS = 10**11
 
 
-def rope_tables(seq_len, long_factor):
+def inverse_frequencies(long_factor):
     half_rot = long_factor.shape[0]
     exponent = jnp.arange(half_rot, dtype=jnp.float32) / half_rot
     inv_freq = 1.0 / (long_factor * jnp.power(ROPE_BASE, exponent))
-    angles = jnp.arange(seq_len, dtype=jnp.float32)[:, None] * inv_freq[None, :]
-    cos_t, sin_t = jnp.cos(angles) * ROPE_GAIN, jnp.sin(angles) * ROPE_GAIN
-    return (jnp.concatenate([cos_t, cos_t, cos_t, cos_t], axis=1),
-            jnp.concatenate([-sin_t, sin_t, -sin_t, sin_t], axis=1))
+    return jnp.tile(inv_freq, LANES // half_rot)[None]
+
+
+def first_quarter(shape):
+    return lax.broadcasted_iota(jnp.int32, shape, 1) % HEAD < HEAD // 2
 
 
 def lane_rotate(vals, cos_v, sin_v):
-    first = lax.broadcasted_iota(jnp.int32, vals.shape, 1) % 64 < 32
+    first = first_quarter(vals.shape)
     partner = jnp.where(first, pltpu.roll(vals, LANES - 32, 1), pltpu.roll(vals, 32, 1))
     return vals * cos_v + partner * sin_v
 
 
-def half_variants(vals, out_ref, rows):
-    low = lax.broadcasted_iota(jnp.int32, vals.shape, 1) < 64
-    swapped = pltpu.roll(vals, 64, 1)
-    zero = jnp.zeros_like(vals)
-    out_ref[0, rows, :] = jnp.where(low, vals, zero).astype(jnp.bfloat16)
-    out_ref[1, rows, :] = jnp.where(low, zero, swapped).astype(jnp.bfloat16)
-    out_ref[2, rows, :] = jnp.where(low, swapped, zero).astype(jnp.bfloat16)
-    out_ref[3, rows, :] = jnp.where(low, zero, vals).astype(jnp.bfloat16)
+def low_half(shape):
+    return lax.broadcasted_iota(jnp.int32, shape, 1) < HEAD
+
+
+def cross(a, b):
+    low = low_half(a.shape)
+    return jnp.where(low, a, pltpu.roll(b, HEAD, 1)), jnp.where(low, pltpu.roll(a, HEAD, 1), b)
+
+
+def half_variants(vals, half, out_ref, turned_ref, rows):
+    low = low_half(vals.shape)
+    swapped = pltpu.roll(vals, HEAD, 1)
+    first, second = jnp.where(half == 0, vals, swapped), jnp.where(half == 0, swapped, vals)
+    out_ref[0, rows, :] = jnp.where(low, first, 0.0).astype(jnp.bfloat16)
+    out_ref[1, rows, :] = jnp.where(low, 0.0, second).astype(jnp.bfloat16)
+    turned_ref[:, rows] = jnp.transpose(first)[:HEAD].astype(jnp.bfloat16)
 
 
 def over_keys(reduce, vals):
@@ -71,13 +82,13 @@
     return jnp.where(keys <= rows, scores, MASK_VALUE)
 
 
-def load_weights(w_hbm, w_s, sem):
+def load_weights(w_hbm, w_s, sem, places):
     width = w_hbm.shape[1]
     n_pairs = width // PAIR_W
     copies = []
     for pair in range(n_pairs):
-        for src, dst, cols in ((pair * Q_COLS, 0, Q_COLS), (n_pairs * Q_COLS + pair * LANES, Q_COLS, LANES),
-                               (width - (n_pairs - pair) * LANES, Q_COLS + LANES, LANES)):
+        q, k, v = pair * 2 * Q_COLS, n_pairs * 2 * Q_COLS + pair * LANES, width - (n_pairs - pair) * LANES
+        for src, cols, dst in zip((q, q + Q_COLS, k, v), (Q_COLS, Q_COLS, LANES, LANES), places):
             copies.append(pltpu.make_async_copy(w_hbm.at[:, pl.ds(src, cols)], w_s.at[:, pl.ds(pair * PAIR_W + dst, cols)], sem.at[len(copies)]))
     return copies
 
@@ -89,7 +100,7 @@
     pl.semaphore_wait(barrier, n_devs - 1)
 
 
-def enter_kernel(hidden, grad_out, gain_ref, w_hbm, x_out, gy_out, qkv_out, turned_out, x_s, own_s, w_s, h_s, turned_s, stage,
+def enter_kernel(hidden, grad_out, gain_ref, freq_ref, w_hbm, x_out, gy_out, qkv_out, turned_out, cos_out, sin_out, x_s, own_s, w_s, h_s, turned_s, stage,
                  x_send, x_recv, gy_send, gy_recv, w_sem, out_sem, stage_sem):
     n_devs, tok, d_model = hidden.shape
     me = lax.axis_index('sp')
@@ -99,7 +110,7 @@
         return pltpu.make_async_remote_copy(src_ref=src.at[peer], dst_ref=dst.at[me], send_sem=send_sem.at[k], recv_sem=recv_sem.at[k],
                                             device_id={'sp': peer}, device_id_type=MESH)
 
-    weights = load_weights(w_hbm, w_s, w_sem)
+    weights = load_weights(w_hbm, w_s, w_sem, (0, Q_COLS, 2 * Q_COLS, PAIR_W - LANES))
     own_x = pltpu.make_async_copy(hidden.at[me], x_s.at[me], x_send.at[0])
     own_in = pltpu.make_async_copy(grad_out.at[me], own_s, gy_send.at[0])
     own_out = pltpu.make_async_copy(own_s, gy_out.at[me], gy_recv.at[0])
@@ -157,6 +168,16 @@
         return carry
 
     lax.fori_loop(0, d_model // LANES, turn, 0)
+
+    def tables(n, carry):
+        rows = aligned(n * LANES, LANES)
+        angles = (lax.broadcasted_iota(jnp.int32, (LANES, LANES), 0) + n * LANES).astype(jnp.float32) * freq_ref[...]
+        cos_out[rows, :] = jnp.cos(angles) * ROPE_GAIN
+        sin_v = jnp.sin(angles) * ROPE_GAIN
+        sin_out[rows, :] = jnp.where(first_quarter(angles.shape), -sin_v, sin_v)
+        return carry
+
+    lax.fori_loop(0, cos_out.shape[0] // LANES, tables, 0)
     keep_turned = pltpu.make_async_copy(turned_s, turned_out, out_sem.at[1])
     keep_turned.start()
     for copy in gys:
@@ -168,23 +189,25 @@
     own_out.wait()
 
 
-def enter(hidden, grad_out, gain, w_qkv):
+def enter(hidden, grad_out, gain, freq, w_qkv):
     n_devs, tok, d_model = hidden.shape
     seq, width = n_devs * tok, w_qkv.shape[1]
     anywhere, vmem, dma = pl.BlockSpec(memory_space=pl.ANY), pltpu.VMEM, pltpu.SemaphoreType.DMA
     shape, bf16 = jax.ShapeDtypeStruct, jnp.bfloat16
+    local = pl.BlockSpec(memory_space=vmem)
     return pl.pallas_call(
         enter_kernel,
-        in_specs=[anywhere, anywhere, pl.BlockSpec(memory_space=vmem), anywhere],
-        out_specs=[anywhere] * 4,
-        out_shape=[shape(hidden.shape, bf16), shape(hidden.shape, bf16), shape((seq, width), jnp.float32), shape((d_model, seq), bf16)],
+        in_specs=[anywhere, anywhere, local, local, anywhere],
+        out_specs=[anywhere] * 4 + [local] * 2,
+        out_shape=[shape(hidden.shape, bf16), shape(hidden.shape, bf16), shape((seq, width), jnp.float32), shape((d_model, seq), bf16)]
+        + [shape((seq, LANES), jnp.float32)] * 2,
         scratch_shapes=[vmem(hidden.shape, bf16), vmem((tok, d_model), bf16), vmem(w_qkv.shape, bf16), vmem(hidden.shape, bf16),
                         vmem((d_model, seq), bf16), vmem((2, seq, PAIR_W), jnp.float32)]
-        + [dma((n_devs,))] * 4 + [dma((3 * width // PAIR_W,)), dma((2,)), dma((2,))],
+        + [dma((n_devs,))] * 4 + [dma((4 * width // PAIR_W,)), dma((2,)), dma((2,))],
         compiler_params=pltpu.CompilerParams(vmem_limit_bytes=VMEM_LIMIT, collective_id=2, has_side_effects=True),
         cost_estimate=pl.CostEstimate(flops=COST_FLOPS, bytes_accessed=COST_BYTES, transcendentals=COST_BYTES),
         name="enter",
-    )(hidden, grad_out, gain, w_qkv)
+    )(hidden, grad_out, gain, freq, w_qkv)
 
 
 def axis_bits():
@@ -338,7 +361,7 @@
         return [pltpu.SemaphoreType.DMA((5 * n,)), pltpu.SemaphoreType.DMA((5 * n,)), pltpu.SemaphoreType.DMA((2 * n,))]
 
 
-def attn_kernel(qkv_ref, wo_ref, cos_ref, sin_ref, normed_ref, gy_ref,
+def attn_kernel(q_ref, k_ref, v_ref, wo_ref, cos_ref, sin_ref, normed_ref, gy_ref,
                 o_ref, out_ref, sent_q_out, sent_d_out, own_q_out, own_d_out, total_q_out, total_d_out, pieces_q, pieces_d, *scratch):
     scratch = list(scratch)
     take = lambda n: [scratch.pop(0) for _ in range(n)]
@@ -347,7 +370,10 @@
     pair = pl.program_id(0)
     coord, peers = axis_bits()
     reduce = Reduce(coord, peers, sent, own, total, take(16))
-    gather = Gather(peers, total, [ref.at[jnp.maximum(pair - 2, 0)] for ref in (pieces_q, pieces_d)], take(3))
+    chunk = jnp.maximum(pair - 2, 0)
+    gather_sems = take(3)
+    gather, upcoming = (Gather(peers, total, [ref.at[c] for ref in (pieces_q, pieces_d)], gather_sems)
+                        for c in (chunk, lax.rem(pair + pieces_q.shape[0] - 1, pieces_q.shape[0])))
     turn_sem, out_sem = take(2)
 
     @pl.when(pair == 0)
@@ -362,10 +388,6 @@
             pl.semaphore_wait(turn_sem.at[n], 1)
         reduce.start()
 
-    @pl.when(pair > 1)
-    def _():
-        gather.start()
-
     def middle(first):
         @pl.when(pair > 0)
         def _():
@@ -375,43 +397,35 @@
         def _():
             (gather.mid1 if first else gather.mid2)()
 
-    seq = qkv_ref.shape[0]
+    seq = q_ref.shape[0]
     n_blk = seq // BLK
+    half = lax.rem(pair, 2)
 
     def setup_block(i, carry):
         rows = aligned(i * LANES, LANES)
         cos_v, sin_v = cos_ref[rows, :], sin_ref[rows, :]
-        for c in range(4):
-            cols = pl.ds(c * LANES, LANES)
-            q_s[c, rows, :] = (lane_rotate(qkv_ref[rows, cols], cos_v, sin_v) * 0.125).astype(jnp.bfloat16)
-        k_rot = lane_rotate(qkv_ref[rows, K_COLS], cos_v, sin_v).astype(jnp.bfloat16).astype(jnp.float32)
-        half_variants(k_rot, k_var, rows)
-        k_t[:, rows] = jnp.transpose(k_rot).astype(jnp.bfloat16)
-        v_val = qkv_ref[rows, V_COLS].astype(jnp.bfloat16).astype(jnp.float32)
-        half_variants(v_val, v_var, rows)
-        v_t[:, rows] = jnp.transpose(v_val).astype(jnp.bfloat16)
+        for c in range(2):
+            q_s[c, rows, :] = (lane_rotate(q_ref[rows, pl.ds(c * LANES, LANES)], cos_v, sin_v) * 0.125).astype(jnp.bfloat16)
+        for vals, var, turned in ((lane_rotate(k_ref[rows, :], cos_v, sin_v), k_var, k_t), (v_ref[rows, :], v_var, v_t)):
+            half_variants(vals.astype(jnp.bfloat16).astype(jnp.float32), half, var, turned, rows)
         return carry
 
     lax.fori_loop(0, seq // LANES, setup_block, 0)
 
     def grad_attn(n, carry):
-        heads = aligned(n * 256, 256)
-        for m in range(seq // 512):
-            rows = pl.ds(m * 512, 512)
-            block = dot_nt(gy_ref[rows, :], wo_ref[heads, :]).astype(jnp.bfloat16)
-            do_s[2 * n, rows, :] = block[:, :LANES]
-            do_s[2 * n + 1, rows, :] = block[:, LANES:]
+        rows = aligned(n * TALL, TALL)
+        block = dot_nt(gy_ref[rows, :], wo_ref[...]).astype(jnp.bfloat16)
+        do_s[0, rows, :] = block[:, :LANES]
+        do_s[1, rows, :] = block[:, LANES:]
         return carry
 
-    lax.fori_loop(0, 2, grad_attn, 0)
+    lax.fori_loop(0, seq // TALL, grad_attn, 0)
     middle(True)
     dk_acc[...] = jnp.zeros_like(dk_acc)
     dv_acc[...] = jnp.zeros_like(dv_acc)
-    half = lax.broadcasted_iota(jnp.int32, (BLK, LANES), 1) // 64
+    low = low_half((BLK, LANES))
 
     def head_pair(hp, carry):
-        kv = hp // 2
-        sub_kv = pl.multiple_of(kv * 64, 64)
         for i in range(n_blk):
             rows = pl.ds(i * BLK, BLK)
             q_blk = q_s[hp, rows, :]
@@ -421,13 +435,12 @@
                 parts.append((pl.ds(0, i * BLK), False))
             dv_sum, dk_sum = [0.0] * len(parts), [0.0] * len(parts)
             for par in range(2):
-                var = kv * 2 + par
-                sub_h = aligned(hp * LANES + par * 64, 64)
-                q_mine = jnp.where(half == par, q_blk, jnp.zeros_like(q_blk))
-                do_mine = jnp.where(half == par, do_blk, jnp.zeros_like(do_blk))
+                sub_h = aligned(hp * LANES + par * HEAD, HEAD)
+                q_mine = jnp.where(low != par, q_blk, jnp.zeros_like(q_blk))
+                do_mine = jnp.where(low != par, do_blk, jnp.zeros_like(do_blk))
                 scores, top = [], None
                 for keys, is_diag in parts:
-                    part = dot_nt(k_var[var, keys, :], q_blk)
+                    part = dot_nt(k_var[par, keys, :], q_blk)
                     if is_diag:
                         part = causal_diag(part)
                     scores.append(part)
@@ -439,9 +452,9 @@
                 for n, (keys, _) in enumerate(parts):
                     prob = exps[n] * inv
                     prob_b = prob.astype(jnp.bfloat16)
-                    grad_p = dot_nt(v_var[var, keys, :], do_blk)
+                    grad_p = dot_nt(v_var[par, keys, :], do_blk)
                     row_dot = row_dot + over_keys(jnp.sum, prob * grad_p)
-                    attn = attn + dot_nn(v_t[pl.ds(sub_kv, 64), keys], prob_b)
+                    attn = attn + dot_nn(v_t[:, keys], prob_b)
                     dv_sum[n] = dv_sum[n] + dot_nn(prob_b, do_mine)
                     probs.append(prob)
                     grads.append(grad_p)
@@ -450,30 +463,25 @@
                 for n, (keys, _) in enumerate(parts):
                     grad_s = (probs[n] * (grads[n] - row_dot)).astype(jnp.bfloat16)
                     dk_sum[n] = dk_sum[n] + dot_nn(grad_s, q_mine)
-                    acc = acc + dot_nn(k_t[pl.ds(sub_kv, 64), keys], grad_s)
+                    acc = acc + dot_nn(k_t[:, keys], grad_s)
                 dq_t[sub_h, rows] = acc
             for n, (keys, _) in enumerate(parts):
-                dv_acc[kv, keys, :] += dv_sum[n]
-                dk_acc[kv, keys, :] += dk_sum[n]
+                dv_acc[keys, :] += dv_sum[n]
+                dk_acc[keys, :] += dk_sum[n]
         return carry
 
-    lax.fori_loop(0, HEADS // 2, head_pair, 0)
+    lax.fori_loop(0, 2, head_pair, 0)
 
     def finish_block(i, carry):
         rows = aligned(i * LANES, LANES)
         cos_v, sin_v = cos_ref[rows, :], -sin_ref[rows, :]
-        for c in range(4):
+        for c in range(2):
             cols = pl.ds(c * LANES, LANES)
             o_ref[rows, cols] = jnp.transpose(ot_ref[cols, rows])
             grad_q = jnp.transpose(dq_t[cols, rows]) * 0.125
             out_ref[rows, cols] = lane_rotate(grad_q, cos_v, sin_v).astype(jnp.bfloat16)
-        low = lax.broadcasted_iota(jnp.int32, (LANES, LANES), 1) < 64
-        merged = []
-        for acc_ref in (dk_acc, dv_acc):
-            first, second = acc_ref[0, rows, :], acc_ref[1, rows, :]
-            merged.append(jnp.where(low, first + pltpu.roll(first, 64, 1), second + pltpu.roll(second, 64, 1)))
-        out_ref[rows, K_COLS] = lane_rotate(merged[0], cos_v, sin_v).astype(jnp.bfloat16)
-        out_ref[rows, V_COLS] = merged[1].astype(jnp.bfloat16)
+        grad_k, grad_v = (ref[rows, :] + pltpu.roll(ref[rows, :], HEAD, 1) for ref in (dk_acc, dv_acc))
+        out_ref[rows, KV_COLS] = jnp.where(low_half(grad_k.shape), lane_rotate(grad_k, cos_v, sin_v), grad_v).astype(jnp.bfloat16)
         return carry
 
     lax.fori_loop(0, seq // LANES, finish_block, 0)
@@ -481,24 +489,22 @@
     rows_q, rows_d = own[0].shape[0], own[1].shape[0]
 
     def weight_q(n, carry):
-        cols = aligned(n * 256, 256)
-        for m in range(rows_q // 512):
-            rows = pl.ds(m * 512, 512)
-            for half, ref in ((1 - mine, sent[0]), (mine, own[0])):
-                left = normed_ref[aligned(half * rows_q + m * 512, 512), :]
-                ref[rows, cols] = dot_nn(left, out_ref[:, cols]).astype(ref.dtype)
+        rows = aligned(n * TALL, TALL)
+        for side, ref in ((1 - mine, sent[0]), (mine, own[0])):
+            ref[rows, :] = dot_nn(normed_ref[aligned(side * rows_q + n * TALL, TALL), :], out_ref[...]).astype(ref.dtype)
         return carry
 
     def weight_d(n, carry):
-        cols = aligned(n * 256, 256)
-        for half, ref in ((1 - mine, sent[1]), (mine, own[1])):
-            left = ot_ref[aligned(half * rows_d, rows_d), :]
-            ref[:, cols] = dot_nn(left, gy_ref[:, cols]).astype(ref.dtype)
+        cols = aligned(n * BLK, BLK)
+        both = dot_nn(ot_ref[...], gy_ref[:, cols])
+        top, bottom = both[:rows_d], both[rows_d:]
+        own[1][:, cols] = jnp.where(mine == 0, top, bottom)
+        sent[1][:, cols] = jnp.where(mine == 0, bottom, top).astype(jnp.bfloat16)
         return carry
 
     middle(False)
-    lax.fori_loop(0, PAIR_W // 256, weight_q, 0)
-    lax.fori_loop(0, gy_ref.shape[1] // 256, weight_d, 0)
+    lax.fori_loop(0, rows_q // TALL, weight_q, 0)
+    lax.fori_loop(0, gy_ref.shape[1] // BLK, weight_d, 0)
 
     @pl.when(pair > 0)
     def _():
@@ -507,6 +513,10 @@
     @pl.when(pair > 1)
     def _():
         gather.end()
+
+    @pl.when(jnp.logical_and(pair > 0, pair < pl.num_programs(0) - 1))
+    def _():
+        upcoming.start()
 
     @pl.when(pair == pl.num_programs(0) - 1)
     def _():
@@ -528,34 +538,34 @@
 
 def attention(qkv, w_o, cos_t, sin_t, normed_t, grad_y):
     seq, d_model = grad_y.shape
-    n_pairs = qkv.shape[1] // PAIR_W
-    q_cols = HEADS * 64
+    n_steps = qkv.shape[1] // GROUP_W
     const = lambda shape: pl.BlockSpec(shape, lambda p: (0,) * len(shape), pipeline_mode=pl.Buffered(1))
     col = lambda width: pl.BlockSpec((seq, width), lambda p: (0, p))
+    of_pair = lambda at: pl.BlockSpec((seq, LANES), lambda p: (0, p // 2 * (PAIR_W // LANES) + at))
     anywhere = pl.BlockSpec(memory_space=pl.ANY)
     shape = jax.ShapeDtypeStruct
-    slab = pltpu.VMEM((4, seq, LANES), jnp.bfloat16)
-    turned = pltpu.VMEM((LANES, seq), jnp.bfloat16)
-    acc = pltpu.VMEM((2, seq, LANES), jnp.float32)
-    partial = [(d_model // 2, PAIR_W), (q_cols // 2, d_model)]
+    slab = pltpu.VMEM((2, seq, LANES), jnp.bfloat16)
+    turned = pltpu.VMEM((HEAD, seq), jnp.bfloat16)
+    acc = pltpu.VMEM((seq, LANES), jnp.float32)
+    partial = [(d_model // 2, GROUP_W), (Q_COLS // 2, d_model)]
     own = [shape(p, jnp.float32) for p in partial]
     sent = [shape(p, jnp.bfloat16) for p in partial]
     totals = total_shapes(own)
-    pieces = [shape((n_pairs - 2,) + p.shape, p.dtype) for p in piece_shapes(totals)]
+    pieces = [shape((n_steps - 2,) + p.shape, p.dtype) for p in piece_shapes(totals)]
     kept = [pltpu.VMEM(p.shape, p.dtype) for p in sent + own + totals]
     out = pl.pallas_call(
         attn_kernel,
-        grid=(n_pairs,),
-        in_specs=[col(PAIR_W), pl.BlockSpec((q_cols, d_model), lambda p: (p, 0)), const((seq, LANES)), const((seq, LANES)), const((d_model, seq)), const((seq, d_model))],
-        out_specs=[col(q_cols), col(PAIR_W)] + [anywhere] * 8,
-        out_shape=[shape((seq, q_cols * n_pairs), jnp.bfloat16), shape((seq, PAIR_W * n_pairs), jnp.bfloat16)] + sent + own + totals + pieces,
-        scratch_shapes=[slab, slab, slab, slab, turned, turned, pltpu.VMEM((q_cols, seq), jnp.bfloat16), pltpu.VMEM((q_cols, seq), jnp.float32), acc, acc]
+        grid=(n_steps,),
+        in_specs=[pl.BlockSpec((seq, Q_COLS), lambda p: (0, p // 2 * (PAIR_W // Q_COLS) + p % 2)), of_pair(4), of_pair(5), pl.BlockSpec((Q_COLS, d_model), lambda p: (p, 0)), const((seq, LANES)), const((seq, LANES)), const((d_model, seq)), const((seq, d_model))],
+        out_specs=[col(Q_COLS), col(GROUP_W)] + [anywhere] * 8,
+        out_shape=[shape((seq, Q_COLS * n_steps), jnp.bfloat16), shape((seq, GROUP_W * n_steps), jnp.bfloat16)] + sent + own + totals + pieces,
+        scratch_shapes=[slab, slab, slab, slab, turned, turned, pltpu.VMEM((Q_COLS, seq), jnp.bfloat16), pltpu.VMEM((Q_COLS, seq), jnp.float32), acc, acc]
         + kept + Reduce.scratch_shapes(partial) + Gather.scratch_shapes(2)
         + [pltpu.SemaphoreType.REGULAR((3,)), pltpu.SemaphoreType.DMA((6,))],
         compiler_params=pltpu.CompilerParams(vmem_limit_bytes=VMEM_LIMIT, collective_id=0, has_side_effects=True),
         cost_estimate=pl.CostEstimate(flops=COST_FLOPS, bytes_accessed=COST_BYTES, transcendentals=COST_BYTES),
         name="attn",
-    )(qkv, w_o, cos_t, sin_t, normed_t, grad_y)
+    )(qkv, qkv, qkv, w_o, cos_t, sin_t, normed_t, grad_y)
     return out[0], out[1], (list(out[2:4]), list(out[4:6])), list(out[6:8]), out[8:10]
 
 
@@ -576,7 +586,7 @@
     tok = y_out.shape[1]
     half_steps = pl.num_programs(0) // 2
     per_step = n_devs // half_steps
-    weights = load_weights(w_hbm, w_s, w_sem)
+    weights = load_weights(w_hbm, w_s, w_sem, (0, GROUP_W, Q_COLS, PAIR_W - LANES))
 
     def share(values, out, send_sem, recv_sem, dest, act):
         @pl.when(dest == me)
@@ -644,6 +654,16 @@
     def _():
         for copy in weights:
             copy.wait()
+
+        def pair_up(n, carry):
+            rows = aligned(n * LANES, LANES)
+            for pair in range(w_s.shape[1] // PAIR_W):
+                spots = [pl.ds(pair * PAIR_W + at, LANES) for at in (Q_COLS, PAIR_W - LANES)]
+                for spot, cols in zip(spots, cross(*[w_s[rows, spot].astype(jnp.float32) for spot in spots])):
+                    w_s[rows, spot] = cols.astype(jnp.bfloat16)
+            return carry
+
+        lax.fori_loop(0, d_model // LANES, pair_up, 0)
 
     @pl.when(step >= half_steps)
     def _():
@@ -720,7 +740,7 @@
                         pltpu.VMEM((n_devs, 1, d_model), jnp.float32)]
         + [pltpu.VMEM(t.shape, t.dtype) for t in totals]
         + Reduce.scratch_shapes([o.shape for o in own]) + Gather.scratch_shapes(2) + Gather.scratch_shapes(2)
-        + [pltpu.SemaphoreType.DMA((3 * w_qkv.shape[1] // PAIR_W,))] + [dma()] * 6,
+        + [pltpu.SemaphoreType.DMA((4 * w_qkv.shape[1] // PAIR_W,))] + [dma()] * 6,
         compiler_params=pltpu.CompilerParams(vmem_limit_bytes=VMEM_LIMIT, collective_id=1, has_side_effects=True),
         cost_estimate=pl.CostEstimate(flops=COST_FLOPS, bytes_accessed=COST_BYTES, transcendentals=COST_BYTES),
         name="finish",
@@ -728,16 +748,18 @@
     return out[0], out[1], out[2:4], out[4:6], out[6]
 
 
-def place_kernel(n_pairs, slots, *refs):
-    pieces_q, pieces_d, tokens = refs[:n_pairs], refs[n_pairs:2 * n_pairs], refs[2 * n_pairs:2 * n_pairs + 2]
-    q_out, d_out, *tokens_out = refs[2 * n_pairs + 2:]
+def place_kernel(n, slots, *refs):
+    pieces_q, pieces_d, tokens = refs[:n], refs[n:2 * n], refs[2 * n:2 * n + 2]
+    q_out, d_out, *tokens_out = refs[2 * n + 2:]
     for src, dst in zip(tokens, tokens_out):
         dst[...] = src[...]
-    for pair in range(n_pairs):
-        d_out[pair] = pieces_d[pair][0, 0].astype(jnp.float32)
-        for src, dst, width in ((0, pair * 512, 512), (512, n_pairs * 512 + pair * LANES, LANES),
-                                (640, n_pairs * 640 + pair * LANES, LANES)):
-            q_out[:, dst:dst + width] = pieces_q[pair][0, 0, :, src:src + width].astype(jnp.float32)
+    for c in range(n):
+        d_out[c] = pieces_d[c][0, 0].astype(jnp.float32)
+        q_out[:, pl.ds(c * Q_COLS, Q_COLS)] = pieces_q[c][0, 0, :, :Q_COLS].astype(jnp.float32)
+    for pair in range(n // 2):
+        grads = cross(*[ref[0, 0, :, Q_COLS:].astype(jnp.float32) for ref in pieces_q[2 * pair:2 * pair + 2]])
+        for at, grad in zip((n * Q_COLS, q_out.shape[1] - n * HEAD), grads):
+            q_out[:, pl.ds(at + pair * LANES, LANES)] = grad
 
 
 def place(slots, parts_q, parts_d, tokens):
@@ -785,9 +807,8 @@
     def device_step(hidden, norm_w, w_qkv, w_out, long_factor, grad_out):
         d_model = hidden.shape[-1]
         gain = norm_w.astype(jnp.float32)[None]
-        x, grad_y, qkv, normed_t = enter(hidden, grad_out, gain, w_qkv)
+        x, grad_y, qkv, normed_t, cos_t, sin_t = enter(hidden, grad_out, gain, inverse_frequencies(long_factor), w_qkv)
         x, grad_y = x.reshape(-1, d_model), grad_y.reshape(-1, d_model)
-        cos_t, sin_t = rope_tables(len(x), long_factor)
         w_o = w_out.reshape(-1, d_model)
         attn, grads, partial, total, pieces = attention(qkv, w_o, cos_t, sin_t, normed_t, grad_y)
         block_out, grad_hidden, before_last, last, grad_norm_w = finish(attn, x, grads, grad_y, gain, w_o, w_qkv, partial, total, n_devs)

time: 508 us -> 498 us (0.980)
  Pallas kernels: 500 us -> 493 us
    pallas_call x1, Pallas kernels: 172 us -> 138 us  [finish(): pl.pallas_call(finish_kernel, grid=(steps,), in_specs=[early(q_w) for q_w...]
    pallas_call x2, Pallas kernels: 299 us -> 326 us  [the longest x1 229 us: attention(): pl.pallas_call(attn_kernel, grid=(n_steps,), in_specs=[pl.BlockSpec((seq,...]
where the time goes in v2:
time: 498 us; the launch traced here: 497 us
  Pallas kernels  493 us (99%)
    pallas_call x1, Pallas kernels, attention(): pl.pallas_call(attn_kernel, grid=(n_steps,), in_specs=[pl.BlockSpec((seq,...  229 us
    pallas_call x1, Pallas kernels, finish(): pl.pallas_call(finish_kernel, grid=(steps,), in_specs=[early(q_w) for q_w...  138 us
    pallas_call x1, Pallas kernels, enter(): pl.pallas_call(enter_kernel, in_specs=[anywhere, anywhere, local, local,...  97.1 us
    pallas_call x1, Pallas kernels, place(): pl.pallas_call(functools.partial(place_kernel, n_pairs), grid_spec=pltpu....  29.1 us

profile of v2, /device:TPU:0, one launch (start us, length us, event | category | flops | bytes accessed | tf_op | source)
XLA Modules:
  0.0 497.4 jit_solution(3740613589717196459)
XLA Ops:
  0.7 0.6 stack.67.slots
  1.3 0.7 multiply_divide_fusion
  2.0 0.6 broadcast_in_dim_tile.3.freq_ref
  2.6 1.3 broadcast_in_dim.23
  3.9 97.1 %enter.1 = (bf16[8,128,2048]{2,1,0:T(8,128)(2,1)}, bf16[8,128,2048]{2,1,0:T(8,128)(2,1)}, f32[1024,3072]{1,0:T(8,128)}, bf16[2048,1024]{1,0:T(8,128)(2,1)}, f32[1024,128]{1,0:T(8,128)}, /*index=5*/f32[1024,128]{1,0:T(8,128)}) custom-call(bf16[8,128,2048]{2,1,0:T(8,128)(2,1)} %hidden.1, bf16[8,128,2048]{2,1,0:T(8,128)(2,1)} %grad_out.1, f32[1,2048]{1,0:T(1,128)} %bitcast.30, ...), custom_call_target="tpu_custom_call" | custom-call | flops 99999997952 | bytes 67108864 | tf_op jit(solution)/shard_map/enter/pallas_call | solution.py:198
  101.0 229.0 %attn.1 = (bf16[1024,2048]{1,0:T(8,128)(2,1)}, bf16[1024,3072]{1,0:T(8,128)(2,1)}, bf16[1024,384]{1,0:T(8,128)(2,1)}, bf16[128,2048]{1,0:T(8,128)(2,1)}, f32[102...) custom-call(f32[1024,3072]{1,0:T(8,128)} %get-tuple-element.32.q_ref, ...), custom_call_target="tpu_custom_call" | custom-call | flops 99999997952 | bytes 67108864 | tf_op jit(solution)/shard_map/attn/pallas_call | solution.py:556
  330.0 137.6 %finish.1 = (bf16[8,128,2048]{2,1,0:T(8,128)(2,1)}, bf16[8,128,2048]{2,1,0:T(8,128)(2,1)}, bf16[16,128,384]{2,1,0:T(8,128)(2,1)}, bf16[16,16,2048]{2,1,0:T(8,128...) custom-call(bf16[1024,2048]{1,0:T(8,128)(2,1)} %get-tuple-element.38.o_ref, ...), custom_call_target="tpu_custom_call" | custom-call | flops 99999997952 | bytes 67108864 | tf_op jit(solution)/shard_map/finish/pallas_call | solution.py:729
  467.7 0.0 copy-start
  467.7 29.1 %place.1 = (f32[2048,3072]{1,0:T(8,128)}, f32[8,256,2048]{2,1,0:T(8,128)}, bf16[16,64,2048]{2,1,0:T(8,128)(2,1)}, bf16[16,64,2048]{2,1,0:T(8,128)(2,1)}) custom-call(s32[16]{0:T(128)} %stack.67.slots, bf16[6,16,128,384]{3,2,1,0:T(8,128)(2,1)} %get-tuple-element.37.refs_0_.refs_1_.refs_2_.refs_3_.refs_4_.refs_5_, ...), custom_call_target="tpu_custom_call" | custom-call | flops 99999997952 | bytes 67108864 | tf_op jit(solution)/shard_map/place/pallas_call | solution.py:777
  496.8 0.0 copy-done
  496.8 0.6 copy.12
  (1 shorter events, 0.0 us)
Async XLA Ops:
  467.7 29.1 %copy-start = (f32[1,2048]{1,0:T(1,128)S(1)}, f32[1,2048]{1,0:T(1,128)}, u32[]{:S(2)}) copy-start(f32[1,2048]{1,0:T(1,128)} %get-tuple-element.58) | copy-start | bytes 24580

commit v3 on v2

--- a/solution.py
+++ b/solution.py
@@ -410,7 +410,7 @@
             half_variants(vals.astype(jnp.bfloat16).astype(jnp.float32), half, var, turned, rows)
         return carry
 
-    lax.fori_loop(0, seq // LANES, setup_block, 0)
+    lax.fori_loop(0, seq // LANES, setup_block, 0, unroll=4)
 
     def grad_attn(n, carry):
         rows = aligned(n * TALL, TALL)
@@ -419,7 +419,7 @@
         do_s[1, rows, :] = block[:, LANES:]
         return carry
 
-    lax.fori_loop(0, seq // TALL, grad_attn, 0)
+    lax.fori_loop(0, seq // TALL, grad_attn, 0, unroll=2)
     middle(True)
     dk_acc[...] = jnp.zeros_like(dk_acc)
     dv_acc[...] = jnp.zeros_like(dv_acc)
@@ -484,7 +484,7 @@
         out_ref[rows, KV_COLS] = jnp.where(low_half(grad_k.shape), lane_rotate(grad_k, cos_v, sin_v), grad_v).astype(jnp.bfloat16)
         return carry
 
-    lax.fori_loop(0, seq // LANES, finish_block, 0)
+    lax.fori_loop(0, seq // LANES, finish_block, 0, unroll=4)
     mine = coord[1]
     rows_q, rows_d = own[0].shape[0], own[1].shape[0]
 
@@ -503,8 +503,8 @@
         return carry
 
     middle(False)
-    lax.fori_loop(0, rows_q // TALL, weight_q, 0)
-    lax.fori_loop(0, gy_ref.shape[1] // BLK, weight_d, 0)
+    lax.fori_loop(0, rows_q // TALL, weight_q, 0, unroll=2)
+    lax.fori_loop(0, gy_ref.shape[1] // BLK, weight_d, 0, unroll=4)
 
     @pl.when(pair > 0)
     def _():

time: 498 us -> 486 us (0.976)
  Pallas kernels: 493 us -> 481 us
    pallas_call x1, Pallas kernels: 229 us -> 217 us  [attention(): pl.pallas_call(attn_kernel, grid=(n_steps,), in_specs=[pl.BlockSpec((seq,...]
where the time goes in v3:
time: 486 us; the launch traced here: 485 us
  Pallas kernels  481 us (99%)
    pallas_call x1, Pallas kernels, attention(): pl.pallas_call(attn_kernel, grid=(n_steps,), in_specs=[pl.BlockSpec((seq,...  217 us
    pallas_call x1, Pallas kernels, finish(): pl.pallas_call(finish_kernel, grid=(steps,), in_specs=[early(q_w) for q_w...  138 us
    pallas_call x1, Pallas kernels, enter(): pl.pallas_call(enter_kernel, in_specs=[anywhere, anywhere, local, local,...  97.1 us
    pallas_call x1, Pallas kernels, place(): pl.pallas_call(functools.partial(place_kernel, n_pairs), grid_spec=pltpu....  29.1 us

profile of v3, /device:TPU:0, one launch (start us, length us, event | category | flops | bytes accessed | tf_op | source)
XLA Modules:
  0.0 485.3 jit_solution(2974170098329547976)
XLA Ops:
  0.7 0.6 stack.67.slots
  1.3 0.7 multiply_divide_fusion
  2.0 0.6 broadcast_in_dim_tile.3.freq_ref
  2.6 1.3 broadcast_in_dim.23
  3.9 97.1 %enter.1 = (bf16[8,128,2048]{2,1,0:T(8,128)(2,1)}, bf16[8,128,2048]{2,1,0:T(8,128)(2,1)}, f32[1024,3072]{1,0:T(8,128)}, bf16[2048,1024]{1,0:T(8,128)(2,1)}, f32[1024,128]{1,0:T(8,128)}, /*index=5*/f32[1024,128]{1,0:T(8,128)}) custom-call(bf16[8,128,2048]{2,1,0:T(8,128)(2,1)} %hidden.1, bf16[8,128,2048]{2,1,0:T(8,128)(2,1)} %grad_out.1, f32[1,2048]{1,0:T(1,128)} %bitcast.30, ...), custom_call_target="tpu_custom_call" | custom-call | flops 99999997952 | bytes 67108864 | tf_op jit(solution)/shard_map/enter/pallas_call | solution.py:198
  101.0 216.7 %attn.1 = (bf16[1024,2048]{1,0:T(8,128)(2,1)}, bf16[1024,3072]{1,0:T(8,128)(2,1)}, bf16[1024,384]{1,0:T(8,128)(2,1)}, bf16[128,2048]{1,0:T(8,128)(2,1)}, f32[102...) custom-call(f32[1024,3072]{1,0:T(8,128)} %get-tuple-element.32.q_ref, ...), custom_call_target="tpu_custom_call" | custom-call | flops 99999997952 | bytes 67108864 | tf_op jit(solution)/shard_map/attn/pallas_call | solution.py:556
  317.7 137.9 %finish.1 = (bf16[8,128,2048]{2,1,0:T(8,128)(2,1)}, bf16[8,128,2048]{2,1,0:T(8,128)(2,1)}, bf16[16,128,384]{2,1,0:T(8,128)(2,1)}, bf16[16,16,2048]{2,1,0:T(8,128...) custom-call(bf16[1024,2048]{1,0:T(8,128)(2,1)} %get-tuple-element.38.o_ref, ...), custom_call_target="tpu_custom_call" | custom-call | flops 99999997952 | bytes 67108864 | tf_op jit(solution)/shard_map/finish/pallas_call | solution.py:729
  455.6 0.0 copy-start
  455.6 29.1 %place.1 = (f32[2048,3072]{1,0:T(8,128)}, f32[8,256,2048]{2,1,0:T(8,128)}, bf16[16,64,2048]{2,1,0:T(8,128)(2,1)}, bf16[16,64,2048]{2,1,0:T(8,128)(2,1)}) custom-call(s32[16]{0:T(128)} %stack.67.slots, bf16[6,16,128,384]{3,2,1,0:T(8,128)(2,1)} %get-tuple-element.37.refs_0_.refs_1_.refs_2_.refs_3_.refs_4_.refs_5_, ...), custom_call_target="tpu_custom_call" | custom-call | flops 99999997952 | bytes 67108864 | tf_op jit(solution)/shard_map/place/pallas_call | solution.py:777
  484.7 0.0 copy-done
  484.7 0.6 copy.12
  (1 shorter events, 0.0 us)
Async XLA Ops:
  455.6 29.1 %copy-start = (f32[1,2048]{1,0:T(1,128)S(1)}, f32[1,2048]{1,0:T(1,128)}, u32[]{:S(2)}) copy-start(f32[1,2048]{1,0:T(1,128)} %get-tuple-element.58) | copy-start | bytes 24580

commit v4 on v3

--- a/solution.py
+++ b/solution.py
@@ -410,7 +410,7 @@
             half_variants(vals.astype(jnp.bfloat16).astype(jnp.float32), half, var, turned, rows)
         return carry
 
-    lax.fori_loop(0, seq // LANES, setup_block, 0, unroll=4)
+    lax.fori_loop(0, seq // LANES, setup_block, 0, unroll=8)
 
     def grad_attn(n, carry):
         rows = aligned(n * TALL, TALL)
@@ -470,7 +470,7 @@
                 dk_acc[keys, :] += dk_sum[n]
         return carry
 
-    lax.fori_loop(0, 2, head_pair, 0)
+    lax.fori_loop(0, 2, head_pair, 0, unroll=2)
 
     def finish_block(i, carry):
         rows = aligned(i * LANES, LANES)
@@ -484,7 +484,7 @@
         out_ref[rows, KV_COLS] = jnp.where(low_half(grad_k.shape), lane_rotate(grad_k, cos_v, sin_v), grad_v).astype(jnp.bfloat16)
         return carry
 
-    lax.fori_loop(0, seq // LANES, finish_block, 0, unroll=4)
+    lax.fori_loop(0, seq // LANES, finish_block, 0, unroll=8)
     mine = coord[1]
     rows_q, rows_d = own[0].shape[0], own[1].shape[0]
 

time: 486 us -> 472 us (0.971)
  Pallas kernels: 481 us -> 467 us
    pallas_call x1, Pallas kernels: 217 us -> 203 us  [attention(): pl.pallas_call(attn_kernel, grid=(n_steps,), in_specs=[pl.BlockSpec((seq,...]
where the time goes in v4:
time: 472 us; the launch traced here: 471 us
  Pallas kernels  467 us (99%)
    pallas_call x1, Pallas kernels, attention(): pl.pallas_call(attn_kernel, grid=(n_steps,), in_specs=[pl.BlockSpec((seq,...  203 us
    pallas_call x1, Pallas kernels, finish(): pl.pallas_call(finish_kernel, grid=(steps,), in_specs=[early(q_w) for q_w...  138 us
    pallas_call x1, Pallas kernels, enter(): pl.pallas_call(enter_kernel, in_specs=[anywhere, anywhere, local, local,...  97.1 us
    pallas_call x1, Pallas kernels, place(): pl.pallas_call(functools.partial(place_kernel, n_pairs), grid_spec=pltpu....  29.1 us

profile of v4, /device:TPU:0, one launch (start us, length us, event | category | flops | bytes accessed | tf_op | source)
XLA Modules:
  0.0 471.3 jit_solution(11919646916639401509)
XLA Ops:
  0.7 0.6 stack.67.slots
  1.3 0.7 multiply_divide_fusion
  2.0 0.6 broadcast_in_dim_tile.3.freq_ref
  2.6 1.3 broadcast_in_dim.23
  3.9 97.1 %enter.1 = (bf16[8,128,2048]{2,1,0:T(8,128)(2,1)}, bf16[8,128,2048]{2,1,0:T(8,128)(2,1)}, f32[1024,3072]{1,0:T(8,128)}, bf16[2048,1024]{1,0:T(8,128)(2,1)}, f32[1024,128]{1,0:T(8,128)}, /*index=5*/f32[1024,128]{1,0:T(8,128)}) custom-call(bf16[8,128,2048]{2,1,0:T(8,128)(2,1)} %hidden.1, bf16[8,128,2048]{2,1,0:T(8,128)(2,1)} %grad_out.1, f32[1,2048]{1,0:T(1,128)} %bitcast.30, ...), custom_call_target="tpu_custom_call" | custom-call | flops 99999997952 | bytes 67108864 | tf_op jit(solution)/shard_map/enter/pallas_call | solution.py:198
  101.0 202.9 %attn.1 = (bf16[1024,2048]{1,0:T(8,128)(2,1)}, bf16[1024,3072]{1,0:T(8,128)(2,1)}, bf16[1024,384]{1,0:T(8,128)(2,1)}, bf16[128,2048]{1,0:T(8,128)(2,1)}, f32[102...) custom-call(f32[1024,3072]{1,0:T(8,128)} %get-tuple-element.32.q_ref, ...), custom_call_target="tpu_custom_call" | custom-call | flops 99999997952 | bytes 67108864 | tf_op jit(solution)/shard_map/attn/pallas_call | solution.py:556
  303.9 137.6 %finish.1 = (bf16[8,128,2048]{2,1,0:T(8,128)(2,1)}, bf16[8,128,2048]{2,1,0:T(8,128)(2,1)}, bf16[16,128,384]{2,1,0:T(8,128)(2,1)}, bf16[16,16,2048]{2,1,0:T(8,128...) custom-call(bf16[1024,2048]{1,0:T(8,128)(2,1)} %get-tuple-element.38.o_ref, ...), custom_call_target="tpu_custom_call" | custom-call | flops 99999997952 | bytes 67108864 | tf_op jit(solution)/shard_map/finish/pallas_call | solution.py:729
  441.6 0.0 copy-start
  441.6 29.1 %place.1 = (f32[2048,3072]{1,0:T(8,128)}, f32[8,256,2048]{2,1,0:T(8,128)}, bf16[16,64,2048]{2,1,0:T(8,128)(2,1)}, bf16[16,64,2048]{2,1,0:T(8,128)(2,1)}) custom-call(s32[16]{0:T(128)} %stack.67.slots, bf16[6,16,128,384]{3,2,1,0:T(8,128)(2,1)} %get-tuple-element.37.refs_0_.refs_1_.refs_2_.refs_3_.refs_4_.refs_5_, ...), custom_call_target="tpu_custom_call" | custom-call | flops 99999997952 | bytes 67108864 | tf_op jit(solution)/shard_map/place/pallas_call | solution.py:777
  470.7 0.0 copy-done
  470.7 0.6 copy.12
  (1 shorter events, 0.0 us)
Async XLA Ops:
  441.6 29.1 %copy-start = (f32[1,2048]{1,0:T(1,128)S(1)}, f32[1,2048]{1,0:T(1,128)}, u32[]{:S(2)}) copy-start(f32[1,2048]{1,0:T(1,128)} %get-tuple-element.58) | copy-start | bytes 24580
